TPU v7x, 16 devices: a 4x2x1 block of a 4x4x8 slice. The times are simulated.
16 devices in a mesh: data: 2 (over y, z), tp: 8 (over x, core).
Axes of the slice: x: 4, y: 2, z: 1, core: 2. Of those that a mesh axis runs over, the one named last changes fastest.
The devices are a block of a 4x4x8 slice.
Arguments:
- x: bfloat16 [16384, 8192], P('data', 'tp'), parts along dimension 0
- w: bfloat16 [8192, 2048], P('tp')
- r: bfloat16 [16384, 2048], P('data'), parts along dimension 0
- g: bfloat16 [2048], replicated
Outputs:
- output: bfloat16 [16384, 2048], P('data'), parts along dimension 0
There are 2 independent parts. A program takes and returns all parts, laid end to end along the dimension named above; an argument that names none is the same for every part.
All inputs are finite; a program needn't handle non-finite values.
Results may differ from a plain program's by a relative error of at most 0.0108205.
Values are sent between devices in bfloat16 or wider.
A program may use at most 768 MiB of HBM per device.

v0:
```python
import jax
import jax.numpy as jnp
from jax import lax
from jax.sharding import PartitionSpec as P

EPS = 1e-6


def solution(mesh):
    tp = mesh.shape["tp"]

    def local(x, w, r, g):
        rows = x.shape[0] // tp
        idx = lax.axis_index("tp")
        p = jnp.dot(x, w, preferred_element_type=jnp.float32).astype(jnp.bfloat16)
        y = lax.psum_scatter(p, "tp", scatter_dimension=0, tiled=True)
        rr = lax.dynamic_slice_in_dim(r, idx * rows, rows, axis=0)
        a = rr.astype(jnp.float32) + y.astype(jnp.float32)
        ms = jnp.mean(a * a, axis=-1, keepdims=True)
        zl = (a * lax.rsqrt(ms + EPS) * g.astype(jnp.float32)).astype(jnp.bfloat16)
        return lax.all_gather(zl, "tp", axis=0, tiled=True)

    return jax.shard_map(
        local,
        mesh=mesh,
        in_specs=(P("data", "tp"), P("tp", None), P("data", None), P(None)),
        out_specs=P("data", None),
        check_vma=False,
    )
```

profile of v0, /device:TPU:113, one launch (start us, length us, event | category | flops | bytes accessed | tf_op | source)
XLA Modules:
  0.0 414.6 jit_solution(4874826846163071359)
XLA Ops:
  6.5 0.0 reduce-scatter.2.cloned.1.call-start
  6.6 45.2 %convolution_convert_fusion = bf16[8192,2048]{1,0:T(8,128)(2,1)} fusion(bf16[8192,1024]{1,0:T(8,128)(2,1)} %param.4, bf16[1024,2048]{1,0:T(8,128)(2,1)} %param.5), kind=kOutput, calls=%fused_computation | convolution fusion | flops 34376515584 | bytes 54525952 | tf_op jit(solution)/shard_map/dot_general | solution.py:15
  51.7 0.0 copy-start.1
  51.7 0.1 reduce-scatter.2.cloned.1.call-update
  51.8 0.2 all-gather.2.cloned.1.call-start
  52.0 0.4 copy-done.1
  52.4 168.4 %reduce-scatter.2.cloned.1.call-done = bf16[1024,2048]{1,0:T(8,128)(2,1)} async-done(((bf16[8192,2048]{1,0:T(8,128)(2,1)}), bf16[1024,2048]{1,0:T(8,128)(2,1)}) %reduce-scatter.2.cloned.1.call-update) | async-done | bytes 4194320 | tf_op jit(solution)/shard_map/reduce_scatter | solution.py:16
  220.8 0.0 copy-start
  220.8 5.0 %multiply_reduce_fusion = f32[1024]{0:T(1024)S(1)} fusion(bf16[1024,2048]{1,0:T(8,128)(2,1)} %reduce-scatter.2.cloned.1.call-done, bf16[8192,2048]{1,0:T(8,128)(2,1)} %param.6, s32[]{:T(128)S(6)} %select_n.3), kind=kLoop, calls=%fused_computation.2 | loop fusion | flops 10484736 | bytes 8392708 | tf_op jit(solution)/shard_map/reduce_sum | solution.py:19
  225.9 0.0 copy-done
  225.9 5.5 %multiply_convert_fusion = bf16[1024,2048]{1,0:T(8,128)(2,1)} fusion(bf16[1024,2048]{1,0:T(8,128)(2,1)S(1)} %copy-done, f32[2048]{0:T(1024)S(1)} %convert_element_type.18, f32[1024]{0:T(1024)S(1)} %add_rsqrt_fusion, bf16[8192,2048]{1,0:T(8,128)(2,1)} %param.6, s32[]{:T(128)S(6)} %select_n.3), kind=kLoop, calls=%fused_computation.1 | loop fusion | flops 12582912 | bytes 12595204 | tf_op jit(solution)/shard_map/convert_element_type | solution.py:20
  231.4 0.1 all-gather.2.cloned.1.call-update
  231.5 153.3 %all-gather.2.cloned.1.call-done = bf16[8192,2048]{1,0:T(8,128)(2,1)} async-done(((bf16[1024,2048]{1,0:T(8,128)(2,1)}), bf16[8192,2048]{1,0:T(8,128)(2,1)}) %all-gather.2.cloned.1.call-update) | async-done | bytes 33554448 | tf_op jit(solution)/shard_map/all_gather | solution.py:21
  384.8 22.9 %copy.6 = bf16[8192,2048]{1,0:T(8,128)(2,1)} copy(bf16[8192,2048]{1,0:T(8,128)(2,1)} %all-gather.2.cloned.1.call-done) | data formatting | bytes 67108864
  (2 shorter events, 0.0 us)
Async XLA Ops:
  6.5 214.3 %reduce-scatter.2.cloned.1.call-start = ((), (), s32[]{:S(2)}) async-start(), calls=%async_computation.1 | async-start | bytes 37748736 | tf_op jit(solution)/shard_map/reduce_scatter | solution.py:16
  51.7 0.7 copy-start.1
  51.8 333.0 %all-gather.2.cloned.1.call-start = ((), (), s32[]{:S(2)}) async-start(), calls=%async_computation.2 | async-start | bytes 37748736 | tf_op jit(solution)/shard_map/all_gather | solution.py:21
  220.8 5.0 %copy-start = (bf16[1024,2048]{1,0:T(8,128)(2,1)S(1)}, bf16[1024,2048]{1,0:T(8,128)(2,1)}, u32[]{:S(2)}) copy-start(bf16[1024,2048]{1,0:T(8,128)(2,1)} %reduce-scatter.2.cloned.1.call-done) | copy-start | bytes 12582916
Sparse Core Ops, SparseCore 0:
  51.9 168.8 reduce-scatter.1
  231.6 153.1 all-gather.1
where the time goes:
time: 415 us
  waiting for transfers between devices  322 us (78%)
  matrix products  45.2 us (11%)
  local copies, waits for them, and re-layouts  23.3 us (6%)
  between operations  13.4 us (3%)
  other arithmetic  10.6 us (3%)
    reduce_scatter x1, waiting for transfers between devices, local(): y = lax.psum_scatter(p, 'tp', scatter_dimension=0, tiled=True)  168 us
    all_gather x1, waiting for transfers between devices, local(): return lax.all_gather(zl, 'tp', axis=0, tiled=True)  153 us
    dot_general x1, matrix products, local(): p = jnp.dot(x, w, preferred_element_type=jnp.float32).astype(jnp.bfloat16)  45.2 us
    unnamed x5, local copies, waits for them, and re-layouts  23.3 us
  transfers between devices with their start and end apart: 2, of which 2 were waited for; matrix products, arithmetic and copies ran while one was open for 0% of the time, Pallas kernels for 0%

commit v1 on v0

v1 whole, which is shorter than its diff:
```python
import functools

import jax
import jax.numpy as jnp
from jax import lax
from jax.experimental import pallas as pl
from jax.experimental.pallas import tpu as pltpu
from jax.sharding import PartitionSpec as P

EPS = 1e-6
MESH = pl.DeviceIdType.MESH
CHIPS = 4
NW = 4
NC = 4
NS = 2
SLOTS = 4


def ring_kernel(
    x, w, r, g, z,
    w_own, w_par, xt, xp, far, near1, stage, rt,
    w_sem, xt_sem, rt_sem,
    wx_send, wx_recv, xp_send, xp_recv,
    st_send, far_recv, near_recv,
    own_send, ag_recv, fwd_send, fwd_recv, d_send, d_recv,
):
    me = lax.axis_index("tp")
    k = lax.rem(me, 2)
    c = lax.div(me, 2)
    chip = lambda d: lax.rem(c + d, CHIPS)
    mine = lambda d: chip(d) * 2 + k
    other = lambda d: chip(d) * 2 + 1 - k
    partner = c * 2 + 1 - k
    to = (mine(1), mine(3))
    NEAR = (1, 3)
    rw, kd = x.shape[3], x.shape[4]
    hid = w.shape[1]
    cw = hid // NC
    sr = rw // NS

    def remote(src, dst, ssem, rsem, dev):
        return pltpu.make_async_remote_copy(
            src_ref=src, dst_ref=dst, send_sem=ssem, recv_sem=rsem,
            device_id={"tp": dev}, device_id_type=MESH,
        )

    def cols(j):
        return pl.ds(pl.multiple_of(j * cw, cw), cw)

    def w_local(j):
        return pltpu.make_async_copy(w.at[:, cols(j)], w_own.at[j], w_sem.at[j])

    def w_remote(j):
        return remote(w.at[:, cols(j)], w_par.at[j], wx_send.at[j], wx_recv.at[j], partner)

    def x_local(t, d, wv):
        return pltpu.make_async_copy(x.at[mine(d), :, wv], xt.at[t], xt_sem.at[t])

    def x_remote(e, d, wv):
        return remote(
            x.at[other(d), :, wv], xp.at[e, wv], xp_send.at[e, wv], xp_recv.at[e, wv], partner
        )

    def r_local(wv, h):
        return pltpu.make_async_copy(r.at[mine(0), h, wv], rt.at[h], rt_sem.at[h])

    def far_copy(D, slot, wv, j):
        return remote(
            stage.at[D, slot, 0], far.at[D, wv, j],
            st_send.at[D, slot], far_recv.at[D, wv, j], to[D],
        )

    def near_copy(D, slot, wv, j):
        if D == 0:
            dst = z.at[to[0], :, wv, :, cols(j)]
        else:
            dst = near1.at[wv, :, :, cols(j)]
        return remote(stage.at[D, slot], dst, st_send.at[D, slot], near_recv.at[D, wv, j], to[D])

    def rows(s):
        return pl.ds(pl.multiple_of(s * sr, sr), sr)

    def zrow(b, wv, h, s):
        return z.at[b, h, wv, rows(s)]

    def own_copy(D, wv, h, s):
        v = zrow(mine(0), wv, h, s)
        return remote(v, v, own_send.at[D, wv, h, s], ag_recv.at[D, wv, h, s], to[D])

    def ag_landed(D, wv, h, s):
        v = zrow(mine(4 - NEAR[D]), wv, h, s)
        return remote(v, v, own_send.at[D, wv, h, s], ag_recv.at[D, wv, h, s], to[D])

    def fwd_copy(D, wv, s):
        v = zrow(mine(4 - NEAR[D]), wv, D, s)
        return remote(v, v, fwd_send.at[D, wv, s], fwd_recv.at[D, wv, s], to[D])

    def fwd_landed(D, wv, s):
        v = zrow(mine(2), wv, D, s)
        return remote(v, v, fwd_send.at[D, wv, s], fwd_recv.at[D, wv, s], to[D])

    def d2d(e, d, wv, h, s):
        v = zrow(mine(d), wv, h, s)
        return remote(v, v, d_send.at[e, wv, h, s], d_recv.at[e, wv, h, s], partner)

    def product(t, e, wv, j):
        a = xt[t].reshape(2 * rw, kd)
        b = xp[e, wv].reshape(2 * rw, kd)
        acc = jnp.dot(a, w_own[j], preferred_element_type=jnp.float32)
        return acc + jnp.dot(b, w_par[j], preferred_element_type=jnp.float32)

    barrier = pltpu.get_barrier_semaphore()
    for dev in (partner, to[0], to[1]):
        pl.semaphore_signal(barrier, inc=1, device_id={"tp": dev}, device_id_type=MESH)
    pl.semaphore_wait(barrier, 3)

    x_local(0, 2, 0).start()
    x_remote(0, 2, 0).start()
    for j in range(NC):
        w_local(j).start()
        w_remote(j).start()
    for wv in range(1, NW):
        x_local(wv, 2, wv).start()
        x_remote(0, 2, wv).start()
    for wv in range(NW):
        for D in range(2):
            x_remote(1 + D, NEAR[D], wv).start()
    for wv in range(NW):
        x_remote(3, 0, wv).start()
    for h in range(2):
        r_local(0, h).start()

    @pl.loop(0, NW)
    def _(wv):
        x_local(wv, 2, wv).wait()
        x_remote(0, 2, wv).wait_recv()

        @pl.loop(0, NC)
        def _(j):
            n = wv * NC + j
            slot = lax.rem(n, SLOTS)

            @pl.when(wv == 0)
            def _():
                w_local(j).wait()
                w_remote(j).wait_recv()

            acc = product(wv, 0, wv, j)
            for D in range(2):

                @pl.when(n >= SLOTS)
                def _():
                    far_copy(D, slot, wv, j).wait_send()

                stage[D, slot, 0] = acc[D * rw : (D + 1) * rw].astype(jnp.bfloat16)
                far_copy(D, slot, wv, j).start()

        D = lax.rem(wv, 2)
        x_local(wv, 1 + 2 * D, lax.div(wv, 2)).start()

    @pl.loop(0, NW)
    def _(wv):
        t0 = lax.rem(2 * wv, 4)
        for D in range(2):
            x_local(t0 + D, NEAR[D], wv).wait()
            x_remote(1 + D, NEAR[D], wv).wait_recv()

        @pl.loop(0, NC)
        def _(j):
            n = wv * NC + j
            slot = lax.rem(n, SLOTS)
            for D in range(2):
                acc = product(t0 + D, 1 + D, wv, j)

                @pl.when(n < SLOTS)
                def _():
                    far_copy(D, slot, wv, j).wait_send()

                @pl.when(n >= SLOTS)
                def _():
                    near_copy(D, slot, wv, j).wait_send()

                far_copy(D, slot, wv, j).wait_recv()
                for h in range(2):
                    part = acc[h * rw : (h + 1) * rw]
                    if h == D:
                        part = part + far[D, wv, j].astype(jnp.float32)
                    stage[D, slot, h] = part.astype(jnp.bfloat16)
                near_copy(D, slot, wv, j).start()

        for D in range(2):

            @pl.when(wv < 2)
            def _():
                x_local(t0 + D, NEAR[D], wv + 2).start()

            @pl.when(wv >= 2)
            def _():
                x_local(t0 + D, 0, 2 * (wv - 2) + D).start()

    @pl.loop(0, NW)
    def _(wv):
        x_local(wv, 0, wv).wait()
        x_remote(3, 0, wv).wait_recv()

        @pl.loop(0, NC)
        def _(j):
            acc = product(wv, 3, wv, j)
            for D in range(2):
                near_copy(D, 0, wv, j).wait_recv()
            for h in range(2):
                y = acc[h * rw : (h + 1) * rw]
                y = y + z[mine(0), h, wv, :, cols(j)].astype(jnp.float32)
                y = y + near1[wv, h, :, cols(j)].astype(jnp.float32)
                z[mine(0), h, wv, :, cols(j)] = y.astype(jnp.bfloat16)

        for h in range(2):
            r_local(wv, h).wait()

            @pl.loop(0, NS)
            def _(s):
                @pl.loop(0, sr // 16)
                def _(i):
                    q = pl.ds(pl.multiple_of(s * sr + i * 16, 16), 16)
                    a = rt[h, q].astype(jnp.float32) + z[mine(0), h, wv, q].astype(jnp.float32)
                    ms = jnp.mean(a * a, axis=-1, keepdims=True)
                    zz = a * lax.rsqrt(ms + EPS) * g[...].astype(jnp.float32)
                    z[mine(0), h, wv, q] = zz.astype(jnp.bfloat16)

                for D in range(2):
                    own_copy(D, wv, h, s).start()
                d2d(0, 0, wv, h, s).start()

            @pl.when(wv < NW - 1)
            def _():
                r_local(wv + 1, h).start()

    @pl.loop(0, NW)
    def _(wv):
        for h in range(2):

            @pl.loop(0, NS)
            def _(s):
                for D in range(2):
                    ag_landed(D, wv, h, s).wait_recv()
                    if h == D:
                        fwd_copy(D, wv, s).start()
                    d2d(1 + D, 4 - NEAR[D], wv, h, s).start()

    @pl.loop(0, NW)
    def _(wv):
        @pl.loop(0, NS)
        def _(s):
            for D in range(2):
                fwd_landed(D, wv, s).wait_recv()
                d2d(3, 2, wv, D, s).start()

    @pl.loop(0, SLOTS)
    def _(slot):
        for D in range(2):
            near_copy(D, slot, 0, 0).wait_send()

    @pl.loop(0, NW)
    def _(wv):
        w_remote(wv).wait_send()
        for e, d in ((0, 2), (1, 1), (2, 3), (3, 0)):
            x_remote(e, d, wv).wait_send()

        @pl.loop(0, NS)
        def _(s):
            for D in range(2):
                for h in range(2):
                    own_copy(D, wv, h, s).wait_send()
                fwd_copy(D, wv, s).wait_send()
            for e, d in ((0, 0), (1, 3), (2, 1), (3, 2)):
                for h in range(2):
                    d2d(e, d, wv, h, s).wait_send()
                    d2d(e, d, wv, h, s).wait_recv()


def store_kernel(z, o, sem):
    n = z.shape[0]
    for i in range(n):
        pltpu.make_async_copy(z.at[i], o.at[i], sem.at[i]).start()
    for i in range(n):
        pltpu.make_async_copy(z.at[i], o.at[i], sem.at[i]).wait()


def solution(mesh):
    tp = mesh.shape["tp"]

    def local(x, w, r, g):
        t, kd = x.shape
        hid = w.shape[1]
        half = t // tp // 2
        rw, cw = half // NW, hid // NC
        x5 = x.reshape(tp, 2, NW, rw, kd)
        r5 = r.reshape(tp, 2, NW, rw, hid)
        dma = pltpu.SemaphoreType.DMA
        bf = jnp.bfloat16
        any_spec = pl.BlockSpec(memory_space=pl.ANY)
        z = pl.pallas_call(
            ring_kernel,
            name="ring",
            out_shape=pltpu.VMEM((tp, 2, NW, rw, hid), bf),
            in_specs=[any_spec, any_spec, any_spec, pl.BlockSpec(memory_space=pltpu.VMEM)],
            out_specs=pl.BlockSpec(memory_space=pltpu.VMEM),
            scratch_shapes=[
                pltpu.VMEM((NC, kd, cw), bf),
                pltpu.VMEM((NC, kd, cw), bf),
                pltpu.VMEM((4, 2, rw, kd), bf),
                pltpu.VMEM((4, NW, 2, rw, kd), bf),
                pltpu.VMEM((2, NW, NC, rw, cw), bf),
                pltpu.VMEM((NW, 2, rw, hid), bf),
                pltpu.VMEM((2, SLOTS, 2, rw, cw), bf),
                pltpu.VMEM((2, rw, hid), bf),
                dma((NC,)), dma((4,)), dma((2,)),
                dma((NC,)), dma((NC,)), dma((4, NW)), dma((4, NW)),
                dma((2, SLOTS)), dma((2, NW, NC)), dma((2, NW, NC)),
                dma((2, NW, 2, NS)), dma((2, NW, 2, NS)), dma((2, NW, NS)), dma((2, NW, NS)),
                dma((4, NW, 2, NS)), dma((4, NW, 2, NS)),
            ],
            compiler_params=pltpu.CompilerParams(
                collective_id=0, has_side_effects=True, vmem_limit_bytes=33000000
            ),
        )(x5, w, r5, g.reshape(1, hid))
        out = pl.pallas_call(
            store_kernel,
            name="store",
            out_shape=jax.ShapeDtypeStruct(z.shape, bf),
            in_specs=[pl.BlockSpec(memory_space=pltpu.VMEM)],
            out_specs=any_spec,
            scratch_shapes=[dma((tp,))],
            compiler_params=pltpu.CompilerParams(vmem_limit_bytes=1 << 20),
        )(z)
        return out.reshape(t, hid)

    return jax.shard_map(
        local,
        mesh=mesh,
        in_specs=(P("data", "tp"), P("tp", None), P("data", None), P(None)),
        out_specs=P("data", None),
        check_vma=False,
    )
```

time: 415 us -> 298 us (0.72)
  waiting for transfers between devices: 322 us -> 0 us
  Pallas kernels: 0 us -> 296 us
  matrix products: 45.2 us -> 0 us
  local copies, waits for them, and re-layouts: 23.3 us -> 1.29 us
  between operations: 13.4 us -> 0.01 us
  other arithmetic: 10.6 us -> 0 us
    pallas_call x0 -> x2, Pallas kernels: none -> 296 us  [the longest x1 285 us: local(): pl.pallas_call(ring_kernel, name='ring', out_shape=pltpu.VMEM((tp, 2, NW,...]
    reduce_scatter x1 -> x0, waiting for transfers between devices: 168 us -> none  [local(): y = lax.psum_scatter(p, 'tp', scatter_dimension=0, tiled=True)]
    all_gather x1 -> x0, waiting for transfers between devices: 153 us -> none  [local(): return lax.all_gather(zl, 'tp', axis=0, tiled=True)]
    dot_general x1 -> x0, matrix products: 45.2 us -> none  [local(): p = jnp.dot(x, w, preferred_element_type=jnp.float32).astype(jnp.bfloat16)]
    unnamed x5 -> x0, local copies, waits for them, and re-layouts: 23.3 us -> none
    convert_element_type x2 -> x0, other arithmetic: 5.54 us -> none  [local(): zl = (a * lax.rsqrt(ms + EPS) * g.astype(jnp.float32)).astype(jnp.bfloat16)]
    reduce_sum x1 -> x0, other arithmetic: 5.02 us -> none  [local(): ms = jnp.mean(a * a, axis=-1, keepdims=True)]
  transfers between devices with their start and end apart: 2 -> 0, of which waited for: 2 -> 0; matrix products, arithmetic and copies ran while one was open for 0% -> 0% of each run, Pallas kernels for 0% -> 0%
where the time goes in v1:
time: 298 us; the launch traced here: 297 us
  Pallas kernels  296 us (99%)
    pallas_call x1, Pallas kernels, local(): pl.pallas_call(ring_kernel, name='ring', out_shape=pltpu.VMEM((tp, 2, NW,...  285 us
    pallas_call x1, Pallas kernels, local(): pl.pallas_call(store_kernel, name='store', out_shape=jax.ShapeDtypeStruct...  11 us

profile of v1, /device:TPU:113, one launch (start us, length us, event | category | flops | bytes accessed | tf_op | source)
XLA Modules:
  0.0 297.4 jit_solution(12840227541170263203)
XLA Ops:
  0.0 1.3 reshape.14.g
  1.3 285.1 %ring.1.z = bf16[8,2,4,128,2048]{4,3,2,1,0:T(8,128)(2,1)S(1)} custom-call(bf16[8,2,4,128,1024]{4,3,2,1,0:T(8,128)(2,1)} %bitcast.4, bf16[1024,2048]{1,0:T(8,128)(2,1)} %w.1, bf16[8,2,4,128,2048]{4,3,2,1,0:T(8,128)(2,1)} %bitcast.3, bf16[1,2048]{1,0:T(2,128)(2,1)} %reshape.14.g), custom_call_target="tpu_custom_call" | custom-call | tf_op jit(solution)/shard_map/ring/pallas_call | solution.py:302
  286.4 11.0 %store.1 = bf16[8,2,4,128,2048]{4,3,2,1,0:T(8,128)(2,1)} custom-call(bf16[8,2,4,128,2048]{4,3,2,1,0:T(8,128)(2,1)S(1)} %ring.1.z), custom_call_target="tpu_custom_call" | custom-call | tf_op jit(solution)/shard_map/store/pallas_call | solution.py:327

commit v2 on v1

--- a/solution.py
+++ b/solution.py
@@ -18,8 +18,8 @@
 
 def ring_kernel(
     x, w, r, g, z,
-    w_own, w_par, xt, xp, far, near1, stage, rt,
-    w_sem, xt_sem, rt_sem,
+    gv, w_own, w_par, xt, xp, far, near1, stage, rt,
+    g_sem, w_sem, xt_sem, rt_sem,
     wx_send, wx_recv, xp_send, xp_recv,
     st_send, far_recv, near_recv,
     own_send, ag_recv, fwd_send, fwd_recv, d_send, d_recv,
@@ -99,9 +99,9 @@
         v = zrow(mine(2), wv, D, s)
         return remote(v, v, fwd_send.at[D, wv, s], fwd_recv.at[D, wv, s], to[D])
 
-    def d2d(e, d, wv, h, s):
+    def d2d(d, wv, h, s):
         v = zrow(mine(d), wv, h, s)
-        return remote(v, v, d_send.at[e, wv, h, s], d_recv.at[e, wv, h, s], partner)
+        return remote(v, v, d_send.at[0], d_recv.at[0], partner)
 
     def product(t, e, wv, j):
         a = xt[t].reshape(2 * rw, kd)
@@ -112,23 +112,26 @@
     barrier = pltpu.get_barrier_semaphore()
     for dev in (partner, to[0], to[1]):
         pl.semaphore_signal(barrier, inc=1, device_id={"tp": dev}, device_id_type=MESH)
+    x_local(0, 2, 0).start()
+    for j in range(NC):
+        w_local(j).start()
+    for wv in range(1, NW):
+        x_local(wv, 2, wv).start()
+    for h in range(2):
+        r_local(0, h).start()
+    pltpu.make_async_copy(g, gv, g_sem).start()
     pl.semaphore_wait(barrier, 3)
 
-    x_local(0, 2, 0).start()
     x_remote(0, 2, 0).start()
     for j in range(NC):
-        w_local(j).start()
         w_remote(j).start()
     for wv in range(1, NW):
-        x_local(wv, 2, wv).start()
         x_remote(0, 2, wv).start()
     for wv in range(NW):
         for D in range(2):
             x_remote(1 + D, NEAR[D], wv).start()
     for wv in range(NW):
         x_remote(3, 0, wv).start()
-    for h in range(2):
-        r_local(0, h).start()
 
     @pl.loop(0, NW)
     def _(wv):
@@ -198,6 +201,9 @@
             def _():
                 x_local(t0 + D, 0, 2 * (wv - 2) + D).start()
 
+    pltpu.make_async_copy(g, gv, g_sem).wait()
+    gain = gv[...].astype(jnp.float32).reshape(1, hid)
+
     @pl.loop(0, NW)
     def _(wv):
         x_local(wv, 0, wv).wait()
@@ -224,12 +230,12 @@
                     q = pl.ds(pl.multiple_of(s * sr + i * 16, 16), 16)
                     a = rt[h, q].astype(jnp.float32) + z[mine(0), h, wv, q].astype(jnp.float32)
                     ms = jnp.mean(a * a, axis=-1, keepdims=True)
-                    zz = a * lax.rsqrt(ms + EPS) * g[...].astype(jnp.float32)
+                    zz = a * lax.rsqrt(ms + EPS) * gain
                     z[mine(0), h, wv, q] = zz.astype(jnp.bfloat16)
 
                 for D in range(2):
                     own_copy(D, wv, h, s).start()
-                d2d(0, 0, wv, h, s).start()
+                d2d(0, wv, h, s).start()
 
             @pl.when(wv < NW - 1)
             def _():
@@ -245,15 +251,7 @@
                     ag_landed(D, wv, h, s).wait_recv()
                     if h == D:
                         fwd_copy(D, wv, s).start()
-                    d2d(1 + D, 4 - NEAR[D], wv, h, s).start()
-
-    @pl.loop(0, NW)
-    def _(wv):
-        @pl.loop(0, NS)
-        def _(s):
-            for D in range(2):
-                fwd_landed(D, wv, s).wait_recv()
-                d2d(3, 2, wv, D, s).start()
+                    d2d(4 - NEAR[D], wv, h, s).start()
 
     @pl.loop(0, SLOTS)
     def _(slot):
@@ -262,7 +260,6 @@
 
     @pl.loop(0, NW)
     def _(wv):
-        w_remote(wv).wait_send()
         for e, d in ((0, 2), (1, 1), (2, 3), (3, 0)):
             x_remote(e, d, wv).wait_send()
 
@@ -271,11 +268,24 @@
             for D in range(2):
                 for h in range(2):
                     own_copy(D, wv, h, s).wait_send()
+
+    @pl.loop(0, NC)
+    def _(j):
+        w_remote(j).wait_send()
+
+    @pl.loop(0, NW)
+    def _(wv):
+        @pl.loop(0, NS)
+        def _(s):
+            for D in range(2):
+                fwd_landed(D, wv, s).wait_recv()
+                d2d(2, wv, D, s).start()
                 fwd_copy(D, wv, s).wait_send()
-            for e, d in ((0, 0), (1, 3), (2, 1), (3, 2)):
-                for h in range(2):
-                    d2d(e, d, wv, h, s).wait_send()
-                    d2d(e, d, wv, h, s).wait_recv()
+
+    every = z.at[pl.ds(0, CHIPS)]
+    d2d_all = remote(every, every, d_send.at[0], d_recv.at[0], partner)
+    d2d_all.wait_send()
+    d2d_all.wait_recv()
 
 
 def store_kernel(z, o, sem):
@@ -303,9 +313,10 @@
             ring_kernel,
             name="ring",
             out_shape=pltpu.VMEM((tp, 2, NW, rw, hid), bf),
-            in_specs=[any_spec, any_spec, any_spec, pl.BlockSpec(memory_space=pltpu.VMEM)],
+            in_specs=[any_spec] * 4,
             out_specs=pl.BlockSpec(memory_space=pltpu.VMEM),
             scratch_shapes=[
+                pltpu.VMEM((hid,), bf),
                 pltpu.VMEM((NC, kd, cw), bf),
                 pltpu.VMEM((NC, kd, cw), bf),
                 pltpu.VMEM((4, 2, rw, kd), bf),
@@ -314,16 +325,16 @@
                 pltpu.VMEM((NW, 2, rw, hid), bf),
                 pltpu.VMEM((2, SLOTS, 2, rw, cw), bf),
                 pltpu.VMEM((2, rw, hid), bf),
-                dma((NC,)), dma((4,)), dma((2,)),
+                dma, dma((NC,)), dma((4,)), dma((2,)),
                 dma((NC,)), dma((NC,)), dma((4, NW)), dma((4, NW)),
                 dma((2, SLOTS)), dma((2, NW, NC)), dma((2, NW, NC)),
                 dma((2, NW, 2, NS)), dma((2, NW, 2, NS)), dma((2, NW, NS)), dma((2, NW, NS)),
-                dma((4, NW, 2, NS)), dma((4, NW, 2, NS)),
+                dma((1,)), dma((1,)),
             ],
             compiler_params=pltpu.CompilerParams(
                 collective_id=0, has_side_effects=True, vmem_limit_bytes=33000000
             ),
-        )(x5, w, r5, g.reshape(1, hid))
+        )(x5, w, r5, g)
         out = pl.pallas_call(
             store_kernel,
             name="store",

time: 298 us -> 294 us (0.987)
  no operation moved by 1% of the time
where the time goes in v2:
time: 294 us
  Pallas kernels  294 us (100%)
    pallas_call x1, Pallas kernels, local(): pl.pallas_call(ring_kernel, name='ring', out_shape=pltpu.VMEM((tp, 2, NW,...  283 us
    pallas_call x1, Pallas kernels, local(): pl.pallas_call(store_kernel, name='store', out_shape=jax.ShapeDtypeStruct...  11 us

profile of v2, /device:TPU:113, one launch (start us, length us, event | category | flops | bytes accessed | tf_op | source)
XLA Modules:
  0.0 294.3 jit_solution(11688529486250568086)
XLA Ops:
  0.0 283.3 %ring.1.z = bf16[8,2,4,128,2048]{4,3,2,1,0:T(8,128)(2,1)S(1)} custom-call(bf16[8,2,4,128,1024]{4,3,2,1,0:T(8,128)(2,1)} %bitcast.4, bf16[1024,2048]{1,0:T(8,128)(2,1)} %w.1, bf16[8,2,4,128,2048]{4,3,2,1,0:T(8,128)(2,1)} %bitcast.3, bf16[2048]{0:T(1024)(128)(2,1)} %g.1), custom_call_target="tpu_custom_call" | custom-call | tf_op jit(solution)/shard_map/ring/pallas_call | solution.py:312
  283.3 11.0 %store.1 = bf16[8,2,4,128,2048]{4,3,2,1,0:T(8,128)(2,1)} custom-call(bf16[8,2,4,128,2048]{4,3,2,1,0:T(8,128)(2,1)S(1)} %ring.1.z), custom_call_target="tpu_custom_call" | custom-call | tf_op jit(solution)/shard_map/store/pallas_call | solution.py:338

commit v3 on v2

v3 whole, which is shorter than its diff:
```python
import jax
import jax.numpy as jnp
from jax import lax
from jax.experimental import pallas as pl
from jax.experimental.pallas import tpu as pltpu
from jax.sharding import PartitionSpec as P

EPS = 1e-6
MESH = pl.DeviceIdType.MESH
CHIPS = 4
NW = 4
NC = 4
FS = 2
SLOTS = 4
NEAR = (1, 3)


def ring_kernel(
    x, w, r, g, z, late, last,
    gv, w_own, w_par, xt, xp, pre, far, near1, stage, rt,
    g_sem, w_sem, xt_sem, rt_sem, late_sem,
    wx_send, wx_recv, xp_send, xp_recv, pre_send, pre_recv,
    st_send, far_recv, near_recv,
    own_send, ag_recv, fwd_send, fwd_recv, d_send, d_recv,
):
    me = lax.axis_index("tp")
    k = lax.rem(me, 2)
    c = lax.div(me, 2)
    chip = lambda d: lax.rem(c + d, CHIPS)
    mine = lambda d: chip(d) * 2 + k
    other = lambda d: chip(d) * 2 + 1 - k
    partner = c * 2 + 1 - k
    to = (mine(1), mine(3))
    rw, kd = x.shape[3], x.shape[4]
    hid = w.shape[1]
    cw = hid // NC
    fr = rw // FS
    bf = jnp.bfloat16

    def remote(src, dst, ssem, rsem, dev):
        return pltpu.make_async_remote_copy(
            src_ref=src, dst_ref=dst, send_sem=ssem, recv_sem=rsem,
            device_id={"tp": dev}, device_id_type=MESH,
        )

    def cols(j):
        return pl.ds(pl.multiple_of(j * cw, cw), cw)

    def w_local(j):
        return pltpu.make_async_copy(w.at[:, cols(j)], w_own.at[j], w_sem.at[j])

    def w_remote(j):
        return remote(w.at[:, cols(j)], w_par.at[j], wx_send, wx_recv.at[j], partner)

    def x_local(t, b, wv):
        return pltpu.make_async_copy(x.at[b, :, wv], xt.at[t], xt_sem.at[t])

    def x_remote(e, d, wv):
        q = wv - 1 if e == 0 else (NW - 1 if e < 3 else NW)
        return remote(x.at[other(d), :, wv], xp.at[e * NW + wv - 1], xp_send, xp_recv.at[q], partner)

    def x_landed(first, n, q):
        v = xp.at[pl.ds(first, n)]
        return remote(v, v, xp_send, xp_recv.at[q], partner)

    def pre_copy(j):
        return remote(stage.at[:, j, 1], pre.at[j], pre_send, pre_recv.at[j], partner)

    def r_local(wv, h):
        return pltpu.make_async_copy(r.at[mine(0), h, wv], rt.at[h], rt_sem.at[h])

    def far_copy(D, slot, wv, j):
        return remote(
            stage.at[D, slot, 0], far.at[D, wv, j],
            st_send.at[D, slot], far_recv.at[D, wv], to[D],
        )

    def far_landed(D, wv):
        v = far.at[D, wv]
        return remote(v, v, st_send.at[D, 0], far_recv.at[D, wv], to[D])

    def near_copy(D, slot, wv, j):
        dst = z.at[to[0], :, wv, :, cols(j)] if D == 0 else near1.at[wv, :, :, cols(j)]
        return remote(stage.at[D, slot], dst, st_send.at[D, slot], near_recv.at[D, wv], to[D])

    def near_landed(D, wv):
        v = z.at[mine(0), :, wv] if D == 0 else near1.at[wv]
        return remote(v, v, st_send.at[D, 0], near_recv.at[D, wv], to[D])

    def own_copy(D, wv, h):
        v = z.at[mine(0), h, wv]
        return remote(v, v, own_send, ag_recv.at[D, wv, h], to[D])

    def ag_landed(D, wv, h):
        v = z.at[mine(4 - NEAR[D]), h, wv]
        return remote(v, v, own_send, ag_recv.at[D, wv, h], to[D])

    def fwd_copy(D, wv, s):
        v = z.at[mine(4 - NEAR[D]), D, wv, pl.ds(s * fr, fr)]
        dst = last.at[D] if (wv, s) == (NW - 2, FS - 1) else v
        return remote(v, dst, fwd_send, fwd_recv.at[D, wv, s], to[D])

    def d2d(v, q):
        return remote(v, v, d_send.at[q], d_recv.at[q], partner)

    def late_local(D, i):
        return pltpu.make_async_copy(z.at[chip(4 - NEAR[D]) * 2 + i, D, NW - 1], late.at[i], late_sem)

    def half_product(t, ww, j):
        return jnp.dot(xt[t].reshape(2 * rw, kd), ww[j], preferred_element_type=jnp.float32)

    def product(t, p, j):
        b = xp[p].reshape(2 * rw, kd)
        return half_product(t, w_own, j) + jnp.dot(b, w_par[j], preferred_element_type=jnp.float32)

    barrier = pltpu.get_barrier_semaphore()
    for dev in (partner, to[0], to[1]):
        pl.semaphore_signal(barrier, inc=1, device_id={"tp": dev}, device_id_type=MESH)
    x_local(3, other(2), 0).start()
    w_local(0).start()
    x_local(0, mine(2), 0).start()
    for j in range(1, NC):
        w_local(j).start()
    for wv in range(1, NW - 1):
        x_local(wv, mine(2), wv).start()
    for h in range(2):
        r_local(0, h).start()
    pltpu.make_async_copy(g, gv, g_sem).start()

    x_local(3, other(2), 0).wait()

    @pl.loop(0, NC)
    def _(j):
        w_local(j).wait()
        acc = half_product(3, w_own, j)
        for h in range(2):
            stage[h, j, 1] = acc[h * rw : (h + 1) * rw].astype(bf)

        @pl.when(j == 0)
        def _():
            pl.semaphore_wait(barrier, 3)

        pre_copy(j).start()

    for j in range(NC):
        if j == 1:
            x_remote(0, 2, 1).start()
        w_remote(j).start()
    for wv in range(2, NW):
        x_remote(0, 2, wv).start()
    for wv in range(NW):
        for D in range(2):
            x_remote(1 + D, NEAR[D], wv).start()
    for wv in range(NW):
        x_remote(3, 0, wv).start()
    x_local(3, mine(2), NW - 1).start()
    x_local(0, mine(2), 0).wait()

    @pl.loop(0, NC)
    def _(j):
        acc = half_product(0, w_own, j)
        pre_copy(j).wait_recv()
        for D in range(2):
            part = acc[D * rw : (D + 1) * rw] + pre[j, D].astype(jnp.float32)
            stage[D, j, 0] = part.astype(bf)
            far_copy(D, j, 0, j).start()

    x_local(0, mine(NEAR[0]), 0).start()
    remote(pre, pre, pre_send, pre_recv.at[0], partner).wait_send()

    @pl.loop(1, NW)
    def _(wv):
        x_local(wv, mine(2), wv).wait()
        x_landed(wv - 1, 1, wv - 1).wait_recv()

        @pl.loop(0, NC)
        def _(j):
            slot = j

            @pl.when(wv == 1)
            def _():
                w_remote(j).wait_recv()

            acc = product(wv, wv - 1, j)
            for D in range(2):
                far_copy(D, slot, wv, j).wait_send()
                stage[D, slot, 0] = acc[D * rw : (D + 1) * rw].astype(bf)
                far_copy(D, slot, wv, j).start()

        D = lax.rem(wv, 2)
        x_local(wv, mine(1 + 2 * D), lax.div(wv, 2)).start()

    x_landed(NW - 1, 2 * NW, NW - 1).wait_recv()

    @pl.loop(0, NW)
    def _(wv):
        t0 = lax.rem(2 * wv, 4)
        for D in range(2):
            x_local(t0 + D, mine(NEAR[D]), wv).wait()
            far_landed(D, wv).wait_recv()

        @pl.loop(0, NC)
        def _(j):
            slot = j
            for D in range(2):
                acc = product(t0 + D, (1 + D) * NW - 1 + wv, j)

                @pl.when(wv == 0)
                def _():
                    far_copy(D, slot, wv, j).wait_send()

                @pl.when(wv > 0)
                def _():
                    near_copy(D, slot, wv, j).wait_send()

                for h in range(2):
                    part = acc[h * rw : (h + 1) * rw]
                    if h == D:
                        part = part + far[D, wv, j].astype(jnp.float32)
                    stage[D, slot, h] = part.astype(bf)
                near_copy(D, slot, wv, j).start()

        for D in range(2):

            @pl.when(wv < 2)
            def _():
                x_local(t0 + D, mine(NEAR[D]), wv + 2).start()

            @pl.when(wv >= 2)
            def _():
                x_local(t0 + D, mine(0), 2 * (wv - 2) + D).start()

    pltpu.make_async_copy(g, gv, g_sem).wait()
    gain = gv[...].astype(jnp.float32).reshape(1, hid)
    x_landed(3 * NW - 1, NW, NW).wait_recv()

    @pl.loop(0, NW)
    def _(wv):
        x_local(wv, mine(0), wv).wait()
        for D in range(2):
            near_landed(D, wv).wait_recv()

        @pl.loop(0, NC)
        def _(j):
            acc = product(wv, 3 * NW - 1 + wv, j)
            for h in range(2):
                y = acc[h * rw : (h + 1) * rw]
                y = y + z[mine(0), h, wv, :, cols(j)].astype(jnp.float32)
                y = y + near1[wv, h, :, cols(j)].astype(jnp.float32)
                z[mine(0), h, wv, :, cols(j)] = y.astype(bf)

        for h in range(2):
            r_local(wv, h).wait()

            @pl.loop(0, rw // 16)
            def _(i):
                q = pl.ds(pl.multiple_of(i * 16, 16), 16)
                a = rt[h, q].astype(jnp.float32) + z[mine(0), h, wv, q].astype(jnp.float32)
                ms = jnp.mean(a * a, axis=-1, keepdims=True)
                z[mine(0), h, wv, q] = (a * lax.rsqrt(ms + EPS) * gain).astype(bf)

            for D in range(2):
                own_copy(D, wv, h).start()
            d2d(z.at[mine(0), h, wv], 0).start()

            @pl.when(wv < NW - 1)
            def _():
                r_local(wv + 1, h).start()

    for wv in range(NW):
        for h in range(2):
            for D in range(2):
                ag_landed(D, wv, h).wait_recv()
                if h == D and wv < NW - 1:
                    for s in range(FS):
                        fwd_copy(D, wv, s).start()
                q = 2 if wv < NW - 1 else (1 if h == D else 3)
                d2d(z.at[mine(4 - NEAR[D]), h, wv], q).start()

    def swapped(q, like):
        d2d(like, q).wait_send()
        d2d(like, q).wait_recv()

    swapped(1, z.at[0, :, 0])
    for D in range(2):

        @pl.when(k == D)
        def _():
            for i in range(2):
                late_local(D, i).start()

    @pl.loop(0, SLOTS)
    def _(slot):
        for D in range(2):
            near_copy(D, slot, 0, 0).wait_send()

    remote(xp, xp, xp_send, xp_recv.at[0], partner).wait_send()
    remote(w_par, w_par, wx_send, wx_recv.at[0], partner).wait_send()
    v = z.at[pl.ds(0, 2)]
    remote(v, v, own_send, ag_recv.at[0, 0, 0], partner).wait_send()
    swapped(0, z.at[0])
    swapped(2, z.at[pl.ds(0, 2), :, pl.ds(0, NW - 1)])
    swapped(3, z.at[0, :, 0])
    pltpu.make_async_copy(late, late, late_sem).wait()

    for wv in range(NW - 1):
        for s in range(FS):
            for D in range(2):
                fwd_copy(D, wv, s).wait_recv()
                if (wv, s) != (NW - 2, FS - 1):
                    d2d(z.at[mine(2), D, wv, pl.ds(s * fr, fr)], 4 if wv < NW - 2 else 5).start()
            if (wv, s) == (NW - 2, FS - 2):
                swapped(4, z.at[0, :, pl.ds(0, NW - 2)])
    swapped(5, z.at[0, :, 0, pl.ds(0, (FS - 1) * fr)])
    v = z.at[0, :, pl.ds(0, NW - 1)]
    remote(v, v, fwd_send, fwd_recv.at[0, 0, 0], partner).wait_send()


def store_kernel(z, o, sem):
    n = z.shape[0]
    for i in range(n):
        pltpu.make_async_copy(z.at[i], o.at[i], sem.at[i]).start()
    for i in range(n):
        pltpu.make_async_copy(z.at[i], o.at[i], sem.at[i]).wait()


def late_kernel(o_in, late, late_other, last, last_other, o, late_sem, last_sem):
    me = lax.axis_index("tp")
    k = lax.rem(me, 2)
    chip = lax.rem(lax.div(me, 2) + 2, CHIPS) * 2
    fr = last.shape[1]
    rows = pl.ds((FS - 1) * fr, fr)
    copies = []
    for n in range(2):
        v, u = (late, late_other)[n], (last, last_other)[n]
        core = k if n == 0 else 1 - k
        for i in range(2):
            dst = o.at[chip + i, core, NW - 1]
            copies.append(pltpu.make_async_copy(v.at[i], dst, late_sem.at[n, i]))
            dst = o.at[chip + core, i, NW - 2, rows]
            copies.append(pltpu.make_async_copy(u.at[i], dst, last_sem.at[n, i]))
    for copy in copies:
        copy.start()
    for copy in copies:
        copy.wait()


def solution(mesh):
    tp = mesh.shape["tp"]
    onward = [(i, (i + 2 if i % 2 == 0 else i - 2) % tp) for i in range(tp)]
    swap = [(i, i + 1 - 2 * (i % 2)) for i in range(tp)]

    def local(x, w, r, g):
        t, kd = x.shape
        hid = w.shape[1]
        half = t // tp // 2
        rw, cw = half // NW, hid // NC
        x5 = x.reshape(tp, 2, NW, rw, kd)
        r5 = r.reshape(tp, 2, NW, rw, hid)
        dma = pltpu.SemaphoreType.DMA
        bf = jnp.bfloat16
        any_spec = pl.BlockSpec(memory_space=pl.ANY)
        z, late, last = pl.pallas_call(
            ring_kernel,
            name="ring",
            out_shape=(
                pltpu.VMEM((tp, 2, NW, rw, hid), bf),
                jax.ShapeDtypeStruct((2, rw, hid), bf),
                jax.ShapeDtypeStruct((2, rw // FS, hid), bf),
            ),
            in_specs=[any_spec] * 4,
            out_specs=(pl.BlockSpec(memory_space=pltpu.VMEM), any_spec, any_spec),
            scratch_shapes=[
                pltpu.VMEM((hid,), bf),
                pltpu.VMEM((NC, kd, cw), bf),
                pltpu.VMEM((NC, kd, cw), bf),
                pltpu.VMEM((4, 2, rw, kd), bf),
                pltpu.VMEM((4 * NW - 1, 2, rw, kd), bf),
                pltpu.VMEM((NC, 2, rw, cw), bf),
                pltpu.VMEM((2, NW, NC, rw, cw), bf),
                pltpu.VMEM((NW, 2, rw, hid), bf),
                pltpu.VMEM((2, SLOTS, 2, rw, cw), bf),
                pltpu.VMEM((2, rw, hid), bf),
                dma, dma((NC,)), dma((4,)), dma((2,)), dma,
                dma, dma((NC,)), dma, dma((NW + 1,)), dma, dma((NC,)),
                dma((2, SLOTS)), dma((2, NW)), dma((2, NW)),
                dma, dma((2, NW, 2)), dma, dma((2, NW - 1, FS)), dma((6,)), dma((6,)),
            ],
            compiler_params=pltpu.CompilerParams(
                collective_id=0, has_side_effects=True, vmem_limit_bytes=33000000
            ),
        )(x5, w, r5, g)
        late = lax.ppermute(late, "tp", onward)
        last_other = lax.ppermute(last, "tp", swap)
        out = pl.pallas_call(
            store_kernel,
            name="store",
            out_shape=jax.ShapeDtypeStruct(z.shape, bf),
            in_specs=[pl.BlockSpec(memory_space=pltpu.VMEM)],
            out_specs=any_spec,
            scratch_shapes=[dma((tp,))],
            compiler_params=pltpu.CompilerParams(vmem_limit_bytes=1 << 20),
            cost_estimate=pl.CostEstimate(
                flops=10**10, bytes_accessed=2 * t * hid, transcendentals=0
            ),
        )(z)
        out, late, last_other = lax.optimization_barrier((out, late, last_other))
        out = pl.pallas_call(
            late_kernel,
            name="late",
            out_shape=jax.ShapeDtypeStruct(z.shape, bf),
            in_specs=[any_spec] * 5,
            out_specs=any_spec,
            scratch_shapes=[dma((2, 2)), dma((2, 2))],
            input_output_aliases={0: 0},
            compiler_params=pltpu.CompilerParams(vmem_limit_bytes=1 << 20),
        )(out, late, lax.ppermute(late, "tp", swap), last, last_other)
        return out.reshape(t, hid)

    return jax.shard_map(
        local,
        mesh=mesh,
        in_specs=(P("data", "tp"), P("tp", None), P("data", None), P(None)),
        out_specs=P("data", None),
        check_vma=False,
    )
```

time: 294 us -> 289 us (0.983)
  Pallas kernels: 294 us -> 280 us
  starting transfers between devices: 0 us -> 4.43 us
  waiting for transfers between devices: 0 us -> 3.98 us
    pallas_call x1 -> x2, Pallas kernels: 283 us -> 269 us  [the longest x1 268 us: local(): pl.pallas_call(ring_kernel, name='ring', out_shape=(pltpu.VMEM((tp, 2, NW...]
    ppermute x0 -> x3, starting transfers between devices: none -> 4.43 us  [the longest x1 3.14 us: local(): lax.ppermute(late, 'tp', swap)]
    ppermute x0 -> x3, waiting for transfers between devices: none -> 3.98 us  [the longest x1 2.29 us: local(): lax.ppermute(late, 'tp', swap)]
  transfers between devices with their start and end apart: 0 -> 3, of which waited for: 0 -> 2; matrix products, arithmetic and copies ran while one was open for 0% -> 0% of each run, Pallas kernels for 0% -> 4%
where the time goes in v3:
time: 289 us
  Pallas kernels  280 us (97%)
  starting transfers between devices  4.43 us (2%)
  waiting for transfers between devices  3.98 us (1%)
    pallas_call x1, Pallas kernels, local(): pl.pallas_call(ring_kernel, name='ring', out_shape=(pltpu.VMEM((tp, 2, NW...  268 us
    pallas_call x1, Pallas kernels, local(): pl.pallas_call(store_kernel, name='store', out_shape=jax.ShapeDtypeStruct...  11 us
  transfers between devices with their start and end apart: 3, of which 2 were waited for; matrix products, arithmetic and copies ran while one was open for 0% of the time, Pallas kernels for 4%

profile of v3, /device:TPU:113, one launch (start us, length us, event | category | flops | bytes accessed | tf_op | source)
XLA Modules:
  0.0 288.8 jit_solution(12616885386965697611)
XLA Ops:
  0.0 267.6 %ring.1 = (bf16[8,2,4,128,2048]{4,3,2,1,0:T(8,128)(2,1)S(1)}, bf16[2,128,2048]{2,1,0:T(8,128)(2,1)}, bf16[2,64,2048]{2,1,0:T(8,128)(2,1)}) custom-call(bf16[8,2,4,128,1024]{4,3,2,1,0:T(8,128)(2,1)} %bitcast.4, bf16[1024,2048]{1,0:T(8,128)(2,1)} %w.1, bf16[8,2,4,128,2048]{4,3,2,1,0:T(8,128)(2,1)} %bitcast.3, bf16[2048]{0:T(1024)(128)(2,1)} %g.1), custom_call_target="tpu_custom_call" | custom-call | tf_op jit(solution)/shard_map/ring/pallas_call | solution.py:363
  267.6 0.6 collective-permute-start
  268.3 0.7 collective-permute-start.1
  268.9 0.0 copy-start
  268.9 11.0 %store.1.o_in = bf16[8,2,4,128,2048]{4,3,2,1,0:T(8,128)(2,1)} custom-call(bf16[8,2,4,128,2048]{4,3,2,1,0:T(8,128)(2,1)S(1)} %get-tuple-element.11.z), custom_call_target="tpu_custom_call" | custom-call | flops 10000000000 | bytes 33554432 | tf_op jit(solution)/shard_map/store/pallas_call | solution.py:395
  280.0 0.0 collective-permute-done.1.last_other
  280.0 1.7 collective-permute-done.late
  281.7 3.1 %collective-permute-start.2 = (bf16[2,128,2048]{2,1,0:T(8,128)(2,1)S(1)}, bf16[2,128,2048]{2,1,0:T(8,128)(2,1)S(1)}, u32[]{:S(2)}, u32[]{:S(2)}) collective-permute-start(bf16[2,128,2048]{2,1,0:T(8,128)(2,1)S(1)} %collective-permute-done.late), channel_id=1, source_target_pairs={{0,1},{1,0},{2,3},{3,2},{4,5},{5,4},{6,7},{7,6},{8,9},{9,8},{10,11... | collective-permute-start | bytes 3145736 | tf_op jit(solution)/shard_map/ppermute | solution.py:417
  284.8 2.3 collective-permute-done.2.late_other
  287.1 0.0 copy-done
  287.1 1.7 late.1
Async XLA Ops:
  267.6 14.0 %collective-permute-start = (bf16[2,128,2048]{2,1,0:T(8,128)(2,1)}, bf16[2,128,2048]{2,1,0:T(8,128)(2,1)S(1)}, u32[]{:S(2)}, u32[]{:S(2)}) collective-permute-start(bf16[2,128,2048]{2,1,0:T(8,128)(2,1)} %get-tuple-element.12), channel_id=1, source_target_pairs={{0,2},{1,7},{2,4},{3,1},{4,6},{5,3},{6,0},{7,5},{8,10},{9,15},{10,... | collective-permute-start | bytes 3145736 | tf_op jit(solution)/shard_map/ppermute | solution.py:393
  268.3 11.7 %collective-permute-start.1 = (bf16[2,64,2048]{2,1,0:T(8,128)(2,1)}, bf16[2,64,2048]{2,1,0:T(8,128)(2,1)S(1)}, u32[]{:S(2)}, u32[]{:S(2)}) collective-permute-start(bf16[2,64,2048]{2,1,0:T(8,128)(2,1)} %get-tuple-element.13.last), channel_id=1, source_target_pairs={{0,1},{1,0},{2,3},{3,2},{4,5},{5,4},{6,7},{7,6},{8,9},{9,8},{10,11... | collective-permute-start | bytes 1572872 | tf_op jit(solution)/shard_map/ppermute | solution.py:394
  268.9 18.2 %copy-start = (bf16[2,64,2048]{2,1,0:T(8,128)(2,1)S(1)}, bf16[2,64,2048]{2,1,0:T(8,128)(2,1)}, u32[]{:S(2)}) copy-start(bf16[2,64,2048]{2,1,0:T(8,128)(2,1)} %get-tuple-element.13.last) | copy-start | bytes 1572868
  281.7 5.4 %collective-permute-start.2 = (bf16[2,128,2048]{2,1,0:T(8,128)(2,1)S(1)}, bf16[2,128,2048]{2,1,0:T(8,128)(2,1)S(1)}, u32[]{:S(2)}, u32[]{:S(2)}) collective-permute-start(bf16[2,128,2048]{2,1,0:T(8,128)(2,1)S(1)} %collective-permute-done.late), channel_id=1, source_target_pairs={{0,1},{1,0},{2,3},{3,2},{4,5},{5,4},{6,7},{7,6},{8,9},{9,8},{10,11... | collective-permute-start | bytes 3145736 | tf_op jit(solution)/shard_map/ppermute | solution.py:417

commit v4 on v3

--- a/solution.py
+++ b/solution.py
@@ -5,18 +5,20 @@
 from jax.experimental.pallas import tpu as pltpu
 from jax.sharding import PartitionSpec as P
 
+
 EPS = 1e-6
 MESH = pl.DeviceIdType.MESH
 CHIPS = 4
 NW = 4
 NC = 4
 FS = 2
+SPLIT = 3 / 4
 SLOTS = 4
 NEAR = (1, 3)
 
 
 def ring_kernel(
-    x, w, r, g, z, late, last,
+    x, w, r, g, z, late_a, late_b, last,
     gv, w_own, w_par, xt, xp, pre, far, near1, stage, rt,
     g_sem, w_sem, xt_sem, rt_sem, late_sem,
     wx_send, wx_recv, xp_send, xp_recv, pre_send, pre_recv,
@@ -104,7 +106,12 @@
         return remote(v, v, d_send.at[q], d_recv.at[q], partner)
 
     def late_local(D, i):
-        return pltpu.make_async_copy(z.at[chip(4 - NEAR[D]) * 2 + i, D, NW - 1], late.at[i], late_sem)
+        ra = late_a.shape[1]
+        v = z.at[chip(4 - NEAR[D]) * 2 + i, D, NW - 1]
+        return (
+            pltpu.make_async_copy(v.at[pl.ds(0, ra)], late_a.at[i], late_sem.at[0]),
+            pltpu.make_async_copy(v.at[pl.ds(ra, rw - ra)], late_b.at[i], late_sem.at[1]),
+        )
 
     def half_product(t, ww, j):
         return jnp.dot(xt[t].reshape(2 * rw, kd), ww[j], preferred_element_type=jnp.float32)
@@ -287,7 +294,8 @@
         @pl.when(k == D)
         def _():
             for i in range(2):
-                late_local(D, i).start()
+                for copy in late_local(D, i):
+                    copy.start()
 
     @pl.loop(0, SLOTS)
     def _(slot):
@@ -301,7 +309,8 @@
     swapped(0, z.at[0])
     swapped(2, z.at[pl.ds(0, 2), :, pl.ds(0, NW - 1)])
     swapped(3, z.at[0, :, 0])
-    pltpu.make_async_copy(late, late, late_sem).wait()
+    pltpu.make_async_copy(late_a, late_a, late_sem.at[0]).wait()
+    pltpu.make_async_copy(late_b, late_b, late_sem.at[1]).wait()
 
     for wv in range(NW - 1):
         for s in range(FS):
@@ -324,52 +333,75 @@
         pltpu.make_async_copy(z.at[i], o.at[i], sem.at[i]).wait()
 
 
-def late_kernel(o_in, late, late_other, last, last_other, o, late_sem, last_sem):
-    me = lax.axis_index("tp")
-    k = lax.rem(me, 2)
-    chip = lax.rem(lax.div(me, 2) + 2, CHIPS) * 2
-    fr = last.shape[1]
-    rows = pl.ds((FS - 1) * fr, fr)
-    copies = []
-    for n in range(2):
-        v, u = (late, late_other)[n], (last, last_other)[n]
-        core = k if n == 0 else 1 - k
-        for i in range(2):
-            dst = o.at[chip + i, core, NW - 1]
-            copies.append(pltpu.make_async_copy(v.at[i], dst, late_sem.at[n, i]))
-            dst = o.at[chip + core, i, NW - 2, rows]
-            copies.append(pltpu.make_async_copy(u.at[i], dst, last_sem.at[n, i]))
+def place(copies):
     for copy in copies:
         copy.start()
     for copy in copies:
         copy.wait()
 
 
+def across():
+    me = lax.axis_index("tp")
+    return lax.rem(me, 2), lax.rem(lax.div(me, 2) + 2, CHIPS) * 2
+
+
+def middle_kernel(o_in, late_a, last, last_other, o, sem):
+    k, chip = across()
+    ra, fr = late_a.shape[1], last.shape[1]
+    rows = pl.ds((FS - 1) * fr, fr)
+    copies = []
+    for i in range(2):
+        for n, (src, dst) in enumerate((
+            (late_a.at[i], o.at[chip + i, k, NW - 1, pl.ds(0, ra)]),
+            (last.at[i], o.at[chip + k, i, NW - 2, rows]),
+            (last_other.at[i], o.at[chip + 1 - k, i, NW - 2, rows]),
+        )):
+            copies.append(pltpu.make_async_copy(src, dst, sem.at[n, i]))
+    place(copies)
+
+
+def late_kernel(o_in, late_b, late_a_other, late_b_other, o, sem):
+    k, chip = across()
+    ra, rb = late_a_other.shape[1], late_b.shape[1]
+    copies = []
+    for i in range(2):
+        for n, (src, half, rows) in enumerate((
+            (late_b, k, pl.ds(ra, rb)),
+            (late_a_other, 1 - k, pl.ds(0, ra)),
+            (late_b_other, 1 - k, pl.ds(ra, rb)),
+        )):
+            dst = o.at[chip + i, half, NW - 1, rows]
+            copies.append(pltpu.make_async_copy(src.at[i], dst, sem.at[n, i]))
+    place(copies)
+
+
 def solution(mesh):
     tp = mesh.shape["tp"]
     onward = [(i, (i + 2 if i % 2 == 0 else i - 2) % tp) for i in range(tp)]
     swap = [(i, i + 1 - 2 * (i % 2)) for i in range(tp)]
 
-    def local(x, w, r, g):
+    def body(x, w, r, g):
         t, kd = x.shape
         hid = w.shape[1]
         half = t // tp // 2
         rw, cw = half // NW, hid // NC
+        ra = int(rw * SPLIT)
         x5 = x.reshape(tp, 2, NW, rw, kd)
         r5 = r.reshape(tp, 2, NW, rw, hid)
         dma = pltpu.SemaphoreType.DMA
         bf = jnp.bfloat16
         any_spec = pl.BlockSpec(memory_space=pl.ANY)
-        z, late, last = pl.pallas_call(
+        z, late_a, late_b, last = pl.pallas_call(
             ring_kernel,
             name="ring",
             out_shape=(
                 pltpu.VMEM((tp, 2, NW, rw, hid), bf),
-                jax.ShapeDtypeStruct((2, rw, hid), bf),
+                jax.ShapeDtypeStruct((2, ra, hid), bf),
+                jax.ShapeDtypeStruct((2, rw - ra, hid), bf),
                 jax.ShapeDtypeStruct((2, rw // FS, hid), bf),
             ),
             in_specs=[any_spec] * 4,
-            out_specs=(pl.BlockSpec(memory_space=pltpu.VMEM), any_spec, any_spec),
+            out_specs=(pl.BlockSpec(memory_space=pltpu.VMEM), any_spec, any_spec, any_spec),
             scratch_shapes=[
                 pltpu.VMEM((hid,), bf),
                 pltpu.VMEM((NC, kd, cw), bf),
@@ -381,7 +413,7 @@
                 pltpu.VMEM((NW, 2, rw, hid), bf),
                 pltpu.VMEM((2, SLOTS, 2, rw, cw), bf),
                 pltpu.VMEM((2, rw, hid), bf),
-                dma, dma((NC,)), dma((4,)), dma((2,)), dma,
+                dma, dma((NC,)), dma((4,)), dma((2,)), dma((2,)),
                 dma, dma((NC,)), dma, dma((NW + 1,)), dma, dma((NC,)),
                 dma((2, SLOTS)), dma((2, NW)), dma((2, NW)),
                 dma, dma((2, NW, 2)), dma, dma((2, NW - 1, FS)), dma((6,)), dma((6,)),
@@ -390,7 +422,8 @@
                 collective_id=0, has_side_effects=True, vmem_limit_bytes=33000000
             ),
         )(x5, w, r5, g)
-        late = lax.ppermute(late, "tp", onward)
+        late_a = lax.ppermute(late_a, "tp", onward)
+        late_b = lax.ppermute(late_b, "tp", onward)
         last_other = lax.ppermute(last, "tp", swap)
         out = pl.pallas_call(
             store_kernel,
@@ -404,21 +437,31 @@
                 flops=10**10, bytes_accessed=2 * t * hid, transcendentals=0
             ),
         )(z)
-        out, late, last_other = lax.optimization_barrier((out, late, last_other))
-        out = pl.pallas_call(
-            late_kernel,
-            name="late",
-            out_shape=jax.ShapeDtypeStruct(z.shape, bf),
-            in_specs=[any_spec] * 5,
-            out_specs=any_spec,
-            scratch_shapes=[dma((2, 2)), dma((2, 2))],
-            input_output_aliases={0: 0},
-            compiler_params=pltpu.CompilerParams(vmem_limit_bytes=1 << 20),
-        )(out, late, lax.ppermute(late, "tp", swap), last, last_other)
+        out, late_a, last_other = lax.optimization_barrier((out, late_a, last_other))
+        late_a_other = lax.ppermute(late_a, "tp", swap)
+
+        def in_place(kernel, *args):
+            return pl.pallas_call(
+                kernel,
+                out_shape=jax.ShapeDtypeStruct(z.shape, bf),
+                in_specs=[any_spec] * len(args),
+                out_specs=any_spec,
+                scratch_shapes=[dma((3, 2))],
+                input_output_aliases={0: 0},
+                compiler_params=pltpu.CompilerParams(vmem_limit_bytes=1 << 20),
+                cost_estimate=pl.CostEstimate(
+                    flops=10**9, bytes_accessed=t * hid // 4, transcendentals=0
+                ),
+            )(*args)
+
+        out = in_place(middle_kernel, out, late_a, last, last_other)
+        out, late_b = lax.optimization_barrier((out, late_b))
+        late_b_other = lax.ppermute(late_b, "tp", swap)
+        out = in_place(late_kernel, out, late_b, late_a_other, late_b_other)
         return out.reshape(t, hid)
 
     return jax.shard_map(
-        local,
+        body,
         mesh=mesh,
         in_specs=(P("data", "tp"), P("tp", None), P("data", None), P(None)),
         out_specs=P("data", None),

time: 289 us -> 292 us (1.010)
    ppermute x3 -> x5, starting transfers between devices: 4.43 us -> 6.45 us  [the longest x1 2.07 us: body(): late_b_other = lax.ppermute(late_b, 'tp', swap)]
    pallas_call x3 -> x4, Pallas kernels: 280 us -> 281 us  [the longest x1 268 us: body(): pl.pallas_call(ring_kernel, name='ring', out_shape=(pltpu.VMEM((tp, 2, NW...]
  transfers between devices with their start and end apart: 3 -> 5, of which waited for: 2 -> 2; matrix products, arithmetic and copies ran while one was open for 0% -> 0% of each run, Pallas kernels for 4% -> 4%
where the time goes in v4:
time: 292 us
  Pallas kernels  281 us (96%)
  starting transfers between devices  6.45 us (2%)
  waiting for transfers between devices  4.73 us (2%)
    pallas_call x1, Pallas kernels, body(): pl.pallas_call(ring_kernel, name='ring', out_shape=(pltpu.VMEM((tp, 2, NW...  268 us
    pallas_call x1, Pallas kernels, body(): pl.pallas_call(store_kernel, name='store', out_shape=jax.ShapeDtypeStruct...  11 us
  transfers between devices with their start and end apart: 5, of which 2 were waited for; matrix products, arithmetic and copies ran while one was open for 0% of the time, Pallas kernels for 4%

profile of v4, /device:TPU:113, one launch (start us, length us, event | category | flops | bytes accessed | tf_op | source)
XLA Modules:
  0.0 292.3 jit_solution(13233872448548006684)
XLA Ops:
  0.0 267.6 %ring.1 = (bf16[8,2,4,128,2048]{4,3,2,1,0:T(8,128)(2,1)S(1)}, bf16[2,96,2048]{2,1,0:T(8,128)(2,1)}, bf16[2,32,2048]{2,1,0:T(8,128)(2,1)}, bf16[2,64,2048]{2,1,0:T(8,128)(2,1)}) custom-call(bf16[8,2,4,128,1024]{4,3,2,1,0:T(8,128)(2,1)} %bitcast.4, bf16[1024,2048]{1,0:T(8,128)(2,1)} %w.1, bf16[8,2,4,128,2048]{4,3,2,1,0:T(8,128)(2,1)} %bitcast.3, bf16[2048]{0:T(1024)(128)(2,1)} %g.1), custom_call_target="tpu_custom_call" | custom-call | tf_op jit(solution)/shard_map/ring/pallas_call | solution.py:394
  267.6 1.3 collective-permute-start.1
  268.9 0.8 collective-permute-start
  269.7 0.0 copy-start.1
  269.7 0.0 copy-start
  269.7 11.0 %store.1.o_in = bf16[8,2,4,128,2048]{4,3,2,1,0:T(8,128)(2,1)} custom-call(bf16[8,2,4,128,2048]{4,3,2,1,0:T(8,128)(2,1)S(1)} %get-tuple-element.14.z), custom_call_target="tpu_custom_call" | custom-call | flops 10000000000 | bytes 33554432 | tf_op jit(solution)/shard_map/store/pallas_call | solution.py:428
  280.8 0.0 collective-permute-done.1.last_other
  280.8 0.0 collective-permute-done.late_a
  280.8 1.6 collective-permute-start.3
  282.4 0.0 copy-done.1
  282.4 0.7 collective-permute-start.2
  283.1 0.0 copy-done
  283.1 1.3 shard_map.46.o_in
  284.4 3.6 %collective-permute-done.2.late_b = bf16[2,32,2048]{2,1,0:T(8,128)(2,1)S(1)} collective-permute-done((bf16[2,32,2048]{2,1,0:T(8,128)(2,1)S(1)}, bf16[2,32,2048]{2,1,0:T(8,128)(2,1)S(1)}, u32[]{:S(2)}, u32[]{:S(2)}) %collective-permute-start.2) | collective-permute-done | bytes 262176 | tf_op jit(solution)/shard_map/ppermute | solution.py:426
  287.9 2.1 collective-permute-start.4
  290.0 1.2 collective-permute-done.4.late_b_other
  291.2 0.0 collective-permute-done.3.late_a_other
  291.2 1.1 shard_map.47
Async XLA Ops:
  267.6 13.1 %collective-permute-start.1 = (bf16[2,64,2048]{2,1,0:T(8,128)(2,1)}, bf16[2,64,2048]{2,1,0:T(8,128)(2,1)S(1)}, u32[]{:S(2)}, u32[]{:S(2)}) collective-permute-start(bf16[2,64,2048]{2,1,0:T(8,128)(2,1)} %get-tuple-element.16.last), channel_id=1, source_target_pairs={{0,1},{1,0},{2,3},{3,2},{4,5},{5,4},{6,7},{7,6},{8,9},{9,8},{10,11... | collective-permute-start | bytes 1572872 | tf_op jit(solution)/shard_map/ppermute | solution.py:427
  268.9 11.9 %collective-permute-start = (bf16[2,96,2048]{2,1,0:T(8,128)(2,1)}, bf16[2,96,2048]{2,1,0:T(8,128)(2,1)S(1)}, u32[]{:S(2)}, u32[]{:S(2)}) collective-permute-start(bf16[2,96,2048]{2,1,0:T(8,128)(2,1)} %get-tuple-element.15), channel_id=1, source_target_pairs={{0,2},{1,7},{2,4},{3,1},{4,6},{5,3},{6,0},{7,5},{8,10},{9,15},{10,... | collective-permute-start | bytes 2359304 | tf_op jit(solution)/shard_map/ppermute | solution.py:425
  269.7 12.7 %copy-start.1 = (bf16[2,32,2048]{2,1,0:T(8,128)(2,1)S(1)}, bf16[2,32,2048]{2,1,0:T(8,128)(2,1)}, u32[]{:S(2)}) copy-start(bf16[2,32,2048]{2,1,0:T(8,128)(2,1)} %get-tuple-element.20) | copy-start | bytes 786436
  269.7 13.4 %copy-start = (bf16[2,64,2048]{2,1,0:T(8,128)(2,1)S(1)}, bf16[2,64,2048]{2,1,0:T(8,128)(2,1)}, u32[]{:S(2)}) copy-start(bf16[2,64,2048]{2,1,0:T(8,128)(2,1)} %get-tuple-element.16.last) | copy-start | bytes 1572868
  280.8 10.4 %collective-permute-start.3 = (bf16[2,96,2048]{2,1,0:T(8,128)(2,1)S(1)}, bf16[2,96,2048]{2,1,0:T(8,128)(2,1)S(1)}, u32[]{:S(2)}, u32[]{:S(2)}) collective-permute-start(bf16[2,96,2048]{2,1,0:T(8,128)(2,1)S(1)} %collective-permute-done.late_a), channel_id=1, source_target_pairs={{0,1},{1,0},{2,3},{3,2},{4,5},{5,4},{6,7},{7,6},{8,9},{9,8},{10,11... | collective-permute-start | bytes 2359304 | tf_op jit(solution)/shard_map/ppermute | solution.py:441
  282.4 5.5 %collective-permute-start.2 = (bf16[2,32,2048]{2,1,0:T(8,128)(2,1)S(1)}, bf16[2,32,2048]{2,1,0:T(8,128)(2,1)S(1)}, u32[]{:S(2)}, u32[]{:S(2)}) collective-permute-start(bf16[2,32,2048]{2,1,0:T(8,128)(2,1)S(1)} %copy-done.1), channel_id=1, source_target_pairs={{0,2},{1,7},{2,4},{3,1},{4,6},{5,3},{6,0},{7,5},{8,10},{9,15},{10,... | collective-permute-start | bytes 786440 | tf_op jit(solution)/shard_map/ppermute | solution.py:426
  287.9 3.2 %collective-permute-start.4 = (bf16[2,32,2048]{2,1,0:T(8,128)(2,1)S(1)}, bf16[2,32,2048]{2,1,0:T(8,128)(2,1)S(1)}, u32[]{:S(2)}, u32[]{:S(2)}) collective-permute-start(bf16[2,32,2048]{2,1,0:T(8,128)(2,1)S(1)} %collective-permute-done.2.late_b), channel_id=1, source_target_pairs={{0,1},{1,0},{2,3},{3,2},{4,5},{5,4},{6,7},{7,6},{8,9},{9,8},{10,11... | collective-permute-start | bytes 786440 | tf_op jit(solution)/shard_map/ppermute | solution.py:459

commit v5 on v4

v5 whole, which is shorter than its diff:
```python
import jax
import jax.numpy as jnp
from jax import lax
from jax.experimental import pallas as pl
from jax.experimental.pallas import tpu as pltpu
from jax.sharding import PartitionSpec as P


EPS = 1e-6
MESH = pl.DeviceIdType.MESH
CHIPS = 4
NW = 4
NC = 4
R0, R1, R2, R3 = 192, 288, 368, 480
STEP = 64
SLOTS = 4
FIRST = 128
NEAR = (1, 3)


def ring_kernel(
    x, w, r, g, z, late_a1, late_a2, late_b, last,
    gv, w_own, w_par, xt, xp, pre, far, near1, stage, rt,
    g_sem, w_sem, xt_sem, rt_sem, late_sem,
    wx_send, wx_recv, xp_send, xp_recv, pre_send, pre_recv,
    st_send, far_recv, near_recv,
    own_send, ag_recv, fwd_send, fwd_recv, last_send, last_recv, d_send, d_recv,
):
    me = lax.axis_index("tp")
    k = lax.rem(me, 2)
    c = lax.div(me, 2)
    chip = lambda d: lax.rem(c + d, CHIPS)
    mine = lambda d: chip(d) * 2 + k
    other = lambda d: chip(d) * 2 + 1 - k
    partner = c * 2 + 1 - k
    to = (mine(1), mine(3))
    rw, kd = x.shape[3], x.shape[4]
    half = NW * rw
    ranges = [(lo, min(lo + STEP, R0)) for lo in range(0, R0, STEP)]
    hid = w.shape[1]
    cw = hid // NC
    bf = jnp.bfloat16

    def remote(src, dst, ssem, rsem, dev):
        return pltpu.make_async_remote_copy(
            src_ref=src, dst_ref=dst, send_sem=ssem, recv_sem=rsem,
            device_id={"tp": dev}, device_id_type=MESH,
        )

    def cols(j):
        return pl.ds(pl.multiple_of(j * cw, cw), cw)

    def wave(wv):
        return pl.ds(pl.multiple_of(wv * rw, rw), rw)

    def w_local(j):
        return pltpu.make_async_copy(w.at[:, cols(j)], w_own.at[j], w_sem.at[j])

    def w_local_part(lo, hi, q):
        v = pl.ds(lo, hi - lo)
        return pltpu.make_async_copy(w.at[:, v], w_own.at[0, :, v], w_sem.at[q])

    def w_remote(j):
        return remote(w.at[:, cols(j)], w_par.at[j], wx_send, wx_recv, partner)

    def x_local(t, b, wv):
        return pltpu.make_async_copy(x.at[b, :, wv], xt.at[t], xt_sem.at[t])

    def x_remote(e, d, wv):
        q = wv - 1 if e == 0 else (NW - 1 if e < 3 else NW)
        return remote(x.at[other(d), :, wv], xp.at[e * NW + wv - 1], xp_send, xp_recv.at[q], partner)

    def x_landed(first, n, q):
        v = xp.at[pl.ds(first, n)]
        return remote(v, v, xp_send, xp_recv.at[q], partner)

    def pre_copy(j):
        return remote(stage.at[:, j, 1], pre.at[j], pre_send, pre_recv.at[j], partner)

    def pre_part(lo, hi, q):
        v = pl.ds(lo, hi - lo)
        return remote(stage.at[:, 0, 1, :, v], pre.at[0, :, :, v], pre_send, pre_recv.at[q], partner)

    def r_local(wv, h):
        return pltpu.make_async_copy(r.at[mine(0), h, wv], rt.at[h], rt_sem.at[h])

    def far_copy(D, slot, wv, j):
        return remote(
            stage.at[D, slot, 0], far.at[D, wv, j],
            st_send.at[D, slot], far_recv.at[D, wv], to[D],
        )

    def far_part(D, lo, hi):
        v = pl.ds(lo, hi - lo)
        sems = st_send.at[D, 0], far_recv.at[D, 0]
        return remote(stage.at[D, 0, 0, :, v], far.at[D, 0, 0, :, v], *sems, to[D])

    def far_landed(D, wv):
        v = far.at[D, wv]
        return remote(v, v, st_send.at[D, 0], far_recv.at[D, wv], to[D])

    def near_copy(D, slot, wv, j):
        dst = z.at[to[0], :, wave(wv), cols(j)] if D == 0 else near1.at[wv, :, :, cols(j)]
        return remote(stage.at[D, slot], dst, st_send.at[D, slot], near_recv.at[D, wv], to[D])

    def near_landed(D, wv):
        v = z.at[mine(0), :, wave(wv)] if D == 0 else near1.at[wv]
        return remote(v, v, st_send.at[D, 0], near_recv.at[D, wv], to[D])

    def own_copy(D, wv, h):
        v = z.at[mine(0), h, wave(wv)]
        return remote(v, v, own_send, ag_recv.at[D, wv, h], to[D])

    def ag_landed(D, wv, h):
        v = z.at[mine(4 - NEAR[D]), h, wave(wv)]
        return remote(v, v, own_send, ag_recv.at[D, wv, h], to[D])

    def fwd_copy(D, n):
        lo, hi = ranges[n]
        v = z.at[mine(4 - NEAR[D]), D, pl.ds(lo, hi - lo)]
        return remote(v, v, fwd_send, fwd_recv.at[D, n], to[D])

    def last_copy(D, i):
        v = z.at[chip(4 - NEAR[D]) * 2 + i, D, pl.ds(R0, R1 - R0)]
        return remote(v, last.at[i, D], last_send, last_recv, to[D])

    def d2d(v, q):
        return remote(v, v, d_send.at[q], d_recv.at[q], partner)

    def late_local(D, i):
        src = lambda D, lo, hi: z.at[chip(4 - NEAR[D]) * 2 + i, D, pl.ds(lo, hi - lo)]
        return (
            pltpu.make_async_copy(src(D, R2, R3), late_a1.at[i], late_sem.at[0]),
            pltpu.make_async_copy(src(D, R3, half), late_a2.at[i], late_sem.at[1]),
            pltpu.make_async_copy(src(1 - D, R1, R2), late_b.at[i], late_sem.at[2]),
        )

    def half_product(t, ww, j):
        return jnp.dot(xt[t].reshape(2 * rw, kd), ww[j], preferred_element_type=jnp.float32)

    def part_product(t, lo, hi):
        a = xt[t].reshape(2 * rw, kd)
        return jnp.dot(a, w_own[0, :, lo:hi], preferred_element_type=jnp.float32)

    def product(t, p, j):
        b = xp[p].reshape(2 * rw, kd)
        return half_product(t, w_own, j) + jnp.dot(b, w_par[j], preferred_element_type=jnp.float32)

    parts = (0, FIRST, 0), (FIRST, cw, NC)
    barrier = pltpu.get_barrier_semaphore()
    for dev in (partner, to[0], to[1]):
        pl.semaphore_signal(barrier, inc=1, device_id={"tp": dev}, device_id_type=MESH)
    x_local(3, other(2), 0).start()
    for part in parts:
        w_local_part(*part).start()
    x_local(0, mine(2), 0).start()
    for j in range(1, NC):
        w_local(j).start()
    for wv in range(1, NW - 1):
        x_local(wv, mine(2), wv).start()
    for h in range(2):
        r_local(0, h).start()
    pltpu.make_async_copy(g, gv, g_sem).start()

    x_local(3, other(2), 0).wait()

    for lo, hi, q in parts:
        w_local_part(lo, hi, q).wait()
        acc = part_product(3, lo, hi)
        for h in range(2):
            stage[h, 0, 1, :, lo:hi] = acc[h * rw : (h + 1) * rw].astype(bf)
        if lo == 0:
            pl.semaphore_wait(barrier, 3)
        pre_part(lo, hi, q).start()

    @pl.loop(1, NC)
    def _(j):
        w_local(j).wait()
        acc = half_product(3, w_own, j)
        for h in range(2):
            stage[h, j, 1] = acc[h * rw : (h + 1) * rw].astype(bf)
        pre_copy(j).start()

    x_local(3, mine(2), NW - 1).start()
    x_local(0, mine(2), 0).wait()

    for lo, hi, q in parts:
        acc = part_product(0, lo, hi)
        pre_part(lo, hi, q).wait_recv()
        for D in range(2):
            part = acc[D * rw : (D + 1) * rw] + pre[0, D, :, lo:hi].astype(jnp.float32)
            stage[D, 0, 0, :, lo:hi] = part.astype(bf)
            far_part(D, lo, hi).start()

    for j in range(NC):
        if j == 1:
            x_remote(0, 2, 1).start()
        w_remote(j).start()
    for wv in range(2, NW):
        x_remote(0, 2, wv).start()
    for wv in range(NW):
        for D in range(2):
            x_remote(1 + D, NEAR[D], wv).start()
    for wv in range(NW):
        x_remote(3, 0, wv).start()

    @pl.loop(1, NC)
    def _(j):
        acc = half_product(0, w_own, j)
        pre_copy(j).wait_recv()
        for D in range(2):
            part = acc[D * rw : (D + 1) * rw] + pre[j, D].astype(jnp.float32)
            stage[D, j, 0] = part.astype(bf)
            far_copy(D, j, 0, j).start()

    x_local(0, mine(NEAR[0]), 0).start()
    remote(pre, pre, pre_send, pre_recv.at[0], partner).wait_send()

    @pl.loop(1, NW)
    def _(wv):
        x_local(wv, mine(2), wv).wait()
        x_landed(wv - 1, 1, wv - 1).wait_recv()

        @pl.when(wv == 1)
        def _():
            remote(w_par, w_par, wx_send, wx_recv, partner).wait_recv()

        @pl.loop(0, NC)
        def _(j):
            slot = j

            acc = product(wv, wv - 1, j)
            for D in range(2):
                far_copy(D, slot, wv, j).wait_send()
                stage[D, slot, 0] = acc[D * rw : (D + 1) * rw].astype(bf)
                far_copy(D, slot, wv, j).start()

        D = lax.rem(wv, 2)
        x_local(wv, mine(1 + 2 * D), lax.div(wv, 2)).start()

    x_landed(NW - 1, 2 * NW, NW - 1).wait_recv()

    @pl.loop(0, NW)
    def _(wv):
        t0 = lax.rem(2 * wv, 4)
        for D in range(2):
            x_local(t0 + D, mine(NEAR[D]), wv).wait()
            far_landed(D, wv).wait_recv()

        @pl.loop(0, NC)
        def _(j):
            slot = j
            for D in range(2):
                acc = product(t0 + D, (1 + D) * NW - 1 + wv, j)

                @pl.when(wv == 0)
                def _():
                    far_copy(D, slot, wv, j).wait_send()

                @pl.when(wv > 0)
                def _():
                    near_copy(D, slot, wv, j).wait_send()

                for h in range(2):
                    part = acc[h * rw : (h + 1) * rw]
                    if h == D:
                        part = part + far[D, wv, j].astype(jnp.float32)
                    stage[D, slot, h] = part.astype(bf)
                near_copy(D, slot, wv, j).start()

        for D in range(2):

            @pl.when(wv < 2)
            def _():
                x_local(t0 + D, mine(NEAR[D]), wv + 2).start()

            @pl.when(wv >= 2)
            def _():
                x_local(t0 + D, mine(0), 2 * (wv - 2) + D).start()

    pltpu.make_async_copy(g, gv, g_sem).wait()
    gain = gv[...].astype(jnp.float32).reshape(1, hid)
    x_landed(3 * NW - 1, NW, NW).wait_recv()

    @pl.loop(0, NW)
    def _(wv):
        x_local(wv, mine(0), wv).wait()
        for D in range(2):
            near_landed(D, wv).wait_recv()

        @pl.loop(0, NC)
        def _(j):
            acc = product(wv, 3 * NW - 1 + wv, j)
            for h in range(2):
                y = acc[h * rw : (h + 1) * rw]
                y = y + z[mine(0), h, wave(wv), cols(j)].astype(jnp.float32)
                y = y + near1[wv, h, :, cols(j)].astype(jnp.float32)
                z[mine(0), h, wave(wv), cols(j)] = y.astype(bf)

        for h in range(2):
            r_local(wv, h).wait()

            @pl.loop(0, rw // 16)
            def _(i):
                q = pl.ds(pl.multiple_of(i * 16, 16), 16)
                p = pl.ds(pl.multiple_of(wv * rw + i * 16, 16), 16)
                a = rt[h, q].astype(jnp.float32) + z[mine(0), h, p].astype(jnp.float32)
                ms = jnp.mean(a * a, axis=-1, keepdims=True)
                z[mine(0), h, p] = (a * lax.rsqrt(ms + EPS) * gain).astype(bf)

            for D in range(2):
                own_copy(D, wv, h).start()
            d2d(z.at[mine(0), h, wave(wv)], 0).start()

            @pl.when(wv < NW - 1)
            def _():
                r_local(wv + 1, h).start()

    for wv in range(NW):
        for h in range(2):
            for D in range(2):
                ag_landed(D, wv, h).wait_recv()
                for n, (lo, hi) in enumerate(ranges):
                    if h == D and lo // rw == wv:
                        fwd_copy(D, n).start()
                d2d(z.at[mine(4 - NEAR[D]), h, wave(wv)], 1).start()

    def swapped(q, like):
        d2d(like, q).wait_send()
        d2d(like, q).wait_recv()

    swapped(1, z.at[pl.ds(0, 2)])

    @pl.when(k == 1)
    def _():
        for D in range(2):
            for i in range(2):
                last_copy(D, i).start()

    for D in range(2):

        @pl.when(k == D)
        def _():
            for i in range(2):
                for copy in late_local(D, i):
                    copy.start()

    @pl.loop(0, SLOTS)
    def _(slot):
        for D in range(2):
            near_copy(D, slot, 0, 0).wait_send()

    remote(xp, xp, xp_send, xp_recv.at[0], partner).wait_send()
    remote(w_par, w_par, wx_send, wx_recv, partner).wait_send()
    v = z.at[pl.ds(0, 2)]
    remote(v, v, own_send, ag_recv.at[0, 0, 0], partner).wait_send()
    swapped(0, z.at[0])
    for n, v in enumerate((late_a1, late_a2, late_b)):
        pltpu.make_async_copy(v, v, late_sem.at[n]).wait()

    for n, (lo, hi) in enumerate(ranges):
        for D in range(2):
            fwd_copy(D, n).wait_recv()
            d2d(z.at[mine(2), D, pl.ds(lo, hi - lo)], 2).start()
    v = z.at[0, :, pl.ds(0, R0)]
    remote(v, v, fwd_send, fwd_recv.at[0, 0], partner).wait_send()
    swapped(2, v)

    @pl.when(k == 1)
    def _():
        remote(last, last, last_send, last_recv, to[0]).wait()


def store_kernel(z, o, sem):
    n = z.shape[0]
    for i in range(n):
        pltpu.make_async_copy(z.at[i], o.at[i], sem.at[i]).start()
    for i in range(n):
        pltpu.make_async_copy(z.at[i], o.at[i], sem.at[i]).wait()


def place(copies):
    for copy in copies:
        copy.start()
    for copy in copies:
        copy.wait()


def across():
    me = lax.axis_index("tp")
    return lax.rem(me, 2), lax.rem(lax.div(me, 2) + 2, CHIPS) * 2


def rows_of(o, b, h, lo, hi):
    return o.at[b, h, pl.ds(lo, hi - lo)]


def last_kernel(o_in, late_b, last, last_other, o, sem):
    k, chip = across()
    rest = [(late_b.at[i], rows_of(o, chip + i, 1 - k, R1, R2)) for i in range(2)]
    for core, v in enumerate((last_other, last)):

        @pl.when(k == core)
        def _():
            pairs = rest + [
                (v.at[i, D], rows_of(o, chip + i, D, R0, R1)) for i in range(2) for D in range(2)
            ]
            place([pltpu.make_async_copy(*p, sem.at[n]) for n, p in enumerate(pairs)])


def middle_kernel(o_in, late_a1, late_b_other, o, sem):
    k, chip = across()
    pairs = []
    for i in range(2):
        pairs.append((late_a1.at[i], rows_of(o, chip + i, k, R2, R3)))
        pairs.append((late_b_other.at[i], rows_of(o, chip + i, k, R1, R2)))
    place([pltpu.make_async_copy(*p, sem.at[n]) for n, p in enumerate(pairs)])


def late_kernel(o_in, late_a2, late_a1_other, late_a2_other, o, sem):
    k, chip = across()
    half = o.shape[2]
    pairs = []
    for i in range(2):
        pairs.append((late_a2.at[i], rows_of(o, chip + i, k, R3, half)))
        pairs.append((late_a1_other.at[i], rows_of(o, chip + i, 1 - k, R2, R3)))
        pairs.append((late_a2_other.at[i], rows_of(o, chip + i, 1 - k, R3, half)))
    place([pltpu.make_async_copy(*p, sem.at[n]) for n, p in enumerate(pairs)])


def solution(mesh):
    tp = mesh.shape["tp"]
    onward = [(i, (i + 2 if i % 2 == 0 else i - 2) % tp) for i in range(tp)]
    back = [(i, (i - 2 if i % 2 == 0 else i + 2) % tp) for i in range(tp)]
    down = [(i + 1, i) for i in range(0, tp, 2)]
    swap = [(i, i + 1 - 2 * (i % 2)) for i in range(tp)]

    def body(x, w, r, g):
        t, kd = x.shape
        hid = w.shape[1]
        half = t // tp // 2
        rw, cw = half // NW, hid // NC
        x5 = x.reshape(tp, 2, NW, rw, kd)
        r5 = r.reshape(tp, 2, NW, rw, hid)
        dma = pltpu.SemaphoreType.DMA
        bf = jnp.bfloat16
        any_spec = pl.BlockSpec(memory_space=pl.ANY)
        z, late_a1, late_a2, late_b, last = pl.pallas_call(
            ring_kernel,
            name="ring",
            out_shape=(
                pltpu.VMEM((tp, 2, half, hid), bf),
                jax.ShapeDtypeStruct((2, R3 - R2, hid), bf),
                jax.ShapeDtypeStruct((2, half - R3, hid), bf),
                jax.ShapeDtypeStruct((2, R2 - R1, hid), bf),
                jax.ShapeDtypeStruct((2, 2, R1 - R0, hid), bf),
            ),
            in_specs=[any_spec] * 4,
            out_specs=(pl.BlockSpec(memory_space=pltpu.VMEM),) + (any_spec,) * 4,
            scratch_shapes=[
                pltpu.VMEM((hid,), bf),
                pltpu.VMEM((NC, kd, cw), bf),
                pltpu.VMEM((NC, kd, cw), bf),
                pltpu.VMEM((4, 2, rw, kd), bf),
                pltpu.VMEM((4 * NW - 1, 2, rw, kd), bf),
                pltpu.VMEM((NC, 2, rw, cw), bf),
                pltpu.VMEM((2, NW, NC, rw, cw), bf),
                pltpu.VMEM((NW, 2, rw, hid), bf),
                pltpu.VMEM((2, SLOTS, 2, rw, cw), bf),
                pltpu.VMEM((2, rw, hid), bf),
                dma, dma((NC + 1,)), dma((4,)), dma((2,)), dma((3,)),
                dma, dma, dma, dma((NW + 1,)), dma, dma((NC + 1,)),
                dma((2, SLOTS)), dma((2, NW)), dma((2, NW)),
                dma, dma((2, NW, 2)), dma, dma((2, -(-R0 // STEP))), dma, dma, dma((3,)), dma((3,)),
            ],
            compiler_params=pltpu.CompilerParams(
                collective_id=0, has_side_effects=True, vmem_limit_bytes=33000000
            ),
        )(x5, w, r5, g)
        late_a1 = lax.ppermute(late_a1, "tp", onward)
        late_b = lax.ppermute(late_b, "tp", back)
        late_a2 = lax.ppermute(late_a2, "tp", onward)
        last_other = lax.ppermute(last, "tp", down)
        out = pl.pallas_call(
            store_kernel,
            name="store",
            out_shape=jax.ShapeDtypeStruct(z.shape, bf),
            in_specs=[pl.BlockSpec(memory_space=pltpu.VMEM)],
            out_specs=any_spec,
            scratch_shapes=[dma((tp,))],
            compiler_params=pltpu.CompilerParams(vmem_limit_bytes=1 << 20),
            cost_estimate=pl.CostEstimate(
                flops=10**10, bytes_accessed=2 * t * hid, transcendentals=0
            ),
        )(z)
        out, late_b, last_other = lax.optimization_barrier((out, late_b, last_other))
        late_b_other = lax.ppermute(late_b, "tp", swap)

        def in_place(kernel, *args):
            return pl.pallas_call(
                kernel,
                out_shape=jax.ShapeDtypeStruct(z.shape, bf),
                in_specs=[any_spec] * len(args),
                out_specs=any_spec,
                scratch_shapes=[dma((6,))],
                input_output_aliases={0: 0},
                compiler_params=pltpu.CompilerParams(vmem_limit_bytes=1 << 20),
                cost_estimate=pl.CostEstimate(
                    flops=10**9, bytes_accessed=t * hid // 4, transcendentals=0
                ),
            )(*args)

        out = in_place(last_kernel, out, late_b, last, last_other)
        out, late_a1 = lax.optimization_barrier((out, late_a1))
        late_a1_other = lax.ppermute(late_a1, "tp", swap)
        out = in_place(middle_kernel, out, late_a1, late_b_other)
        out, late_a2 = lax.optimization_barrier((out, late_a2))
        late_a2_other = lax.ppermute(late_a2, "tp", swap)
        out = in_place(late_kernel, out, late_a2, late_a1_other, late_a2_other)
        return out.reshape(t, hid)

    return jax.shard_map(
        body,
        mesh=mesh,
        in_specs=(P("data", "tp"), P("tp", None), P("data", None), P(None)),
        out_specs=P("data", None),
        check_vma=False,
    )
```

time: 292 us -> 290 us (level)
  Pallas kernels: 281 us -> 274 us
  waiting for transfers between devices: 4.73 us -> 8.57 us
    pallas_call x1, Pallas kernels: 268 us -> 259 us  [body(): pl.pallas_call(ring_kernel, name='ring', out_shape=(pltpu.VMEM((tp, 2, ha...]
    ppermute x4 -> x6, waiting for transfers between devices: 3.57 us -> 8.48 us  [the longest x1 4.23 us: body(): late_a2 = lax.ppermute(late_a2, 'tp', onward)]
    ppermute x4 -> x6, starting transfers between devices: 4.38 us -> 6.88 us  [the longest x1 2.5 us: body(): late_a1 = lax.ppermute(late_a1, 'tp', onward)]
  transfers between devices with their start and end apart: 5 -> 7, of which waited for: 2 -> 4; matrix products, arithmetic and copies ran while one was open for 0% -> 0% of each run, Pallas kernels for 4% -> 5%
where the time goes in v5:
time: 290 us
  Pallas kernels  274 us (94%)
  waiting for transfers between devices  8.57 us (3%)
  starting transfers between devices  6.89 us (2%)
    pallas_call x1, Pallas kernels, body(): pl.pallas_call(ring_kernel, name='ring', out_shape=(pltpu.VMEM((tp, 2, ha...  259 us
    pallas_call x1, Pallas kernels, body(): pl.pallas_call(store_kernel, name='store', out_shape=jax.ShapeDtypeStruct...  11 us
  transfers between devices with their start and end apart: 7, of which 4 were waited for; matrix products, arithmetic and copies ran while one was open for 0% of the time, Pallas kernels for 5%

profile of v5, /device:TPU:113, one launch (start us, length us, event | category | flops | bytes accessed | tf_op | source)
XLA Modules:
  0.0 289.6 jit_solution(5502948873902891311)
XLA Ops:
  0.0 259.3 %ring.1 = (bf16[8,2,512,2048]{3,2,1,0:T(8,128)(2,1)S(1)}, bf16[2,112,2048]{2,1,0:T(8,128)(2,1)}, bf16[2,32,2048]{2,1,0:T(8,128)(2,1)}, bf16[2,80,2048]{2,1,0:T(8,128)(2,1)}, bf16[2,2,96,2048]{3,2,1,0:T(8,128)(2,1)}) custom-call(bf16[8,2,4,128,1024]{4,3,2,1,0:T(8,128)(2,1)} %bitcast.4, bf16[1024,2048]{1,0:T(8,128)(2,1)} %w.1, ...), custom_call_target="tpu_custom_call" | custom-call | tf_op jit(solution)/shard_map/ring/pallas_call | solution.py:448
  259.3 1.4 collective-permute-start.1
  260.7 0.3 collective-permute-start
  260.9 2.5 collective-permute-start.2
  263.4 0.0 copy-start
  263.4 11.0 %store.1.o_in = bf16[8,2,512,2048]{3,2,1,0:T(8,128)(2,1)} custom-call(bf16[8,2,512,2048]{3,2,1,0:T(8,128)(2,1)S(1)} %get-tuple-element.17.z), custom_call_target="tpu_custom_call" | custom-call | flops 10000000000 | bytes 33554432 | tf_op jit(solution)/shard_map/store/pallas_call | solution.py:484
  274.5 0.0 copy-start.1
  274.5 3.1 %collective-permute-done.late_b = bf16[2,80,2048]{2,1,0:T(8,128)(2,1)S(1)} collective-permute-done((bf16[2,80,2048]{2,1,0:T(8,128)(2,1)}, bf16[2,80,2048]{2,1,0:T(8,128)(2,1)S(1)}, u32[]{:S(2)}, u32[]{:S(2)}) %collective-permute-start) | collective-permute-done | bytes 655392 | tf_op jit(solution)/shard_map/ppermute | solution.py:481
  277.6 0.0 collective-permute-done.1.last_other
  277.6 0.0 collective-permute-start.3
  277.6 0.0 copy-done
  277.6 1.4 shard_map.46.o_in
  279.0 0.0 collective-permute-done.2.late_a1
  279.0 0.5 collective-permute-start.5
  279.6 0.0 copy-done.1
  279.6 0.0 collective-permute-start.4
  279.6 0.1 collective-permute-done.3.late_b_other
  279.7 1.2 shard_map.47.o_in
  280.9 4.2 %collective-permute-done.4.late_a2 = bf16[2,32,2048]{2,1,0:T(8,128)(2,1)S(1)} collective-permute-done((bf16[2,32,2048]{2,1,0:T(8,128)(2,1)S(1)}, bf16[2,32,2048]{2,1,0:T(8,128)(2,1)S(1)}, u32[]{:S(2)}, u32[]{:S(2)}) %collective-permute-start.4) | collective-permute-done | bytes 262176 | tf_op jit(solution)/shard_map/ppermute | solution.py:482
  285.1 2.2 collective-permute-start.6
  287.3 1.2 collective-permute-done.6.late_a2_other
  288.4 0.0 collective-permute-done.5.late_a1_other
  288.4 1.1 shard_map.48
Async XLA Ops:
  259.3 18.3 %collective-permute-start.1 = (bf16[2,2,96,2048]{3,2,1,0:T(8,128)(2,1)}, bf16[2,2,96,2048]{3,2,1,0:T(8,128)(2,1)S(1)}, u32[]{:S(2)}, u32[]{:S(2)}) collective-permute-start(bf16[2,2,96,2048]{3,2,1,0:T(8,128)(2,1)} %get-tuple-element.19.last), channel_id=1, source_target_pairs={{1,0},{3,2},{5,4},{7,6},{9,8},{11,10},{13,12},{15,14}} | collective-permute-start | bytes 4718600 | tf_op jit(solution)/shard_map/ppermute | solution.py:483
  260.7 16.9 %collective-permute-start = (bf16[2,80,2048]{2,1,0:T(8,128)(2,1)}, bf16[2,80,2048]{2,1,0:T(8,128)(2,1)S(1)}, u32[]{:S(2)}, u32[]{:S(2)}) collective-permute-start(bf16[2,80,2048]{2,1,0:T(8,128)(2,1)} %get-tuple-element.18), channel_id=1, source_target_pairs={{0,6},{1,3},{2,0},{3,5},{4,2},{5,7},{6,4},{7,1},{8,14},{9,11},{10,... | collective-permute-start | bytes 1966088 | tf_op jit(solution)/shard_map/ppermute | solution.py:481
  260.9 18.1 %collective-permute-start.2 = (bf16[2,112,2048]{2,1,0:T(8,128)(2,1)}, bf16[2,112,2048]{2,1,0:T(8,128)(2,1)S(1)}, u32[]{:S(2)}, u32[]{:S(2)}) collective-permute-start(bf16[2,112,2048]{2,1,0:T(8,128)(2,1)} %get-tuple-element.23), channel_id=1, source_target_pairs={{0,2},{1,7},{2,4},{3,1},{4,6},{5,3},{6,0},{7,5},{8,10},{9,15},{10,... | collective-permute-start | bytes 2752520 | tf_op jit(solution)/shard_map/ppermute | solution.py:480
  263.4 14.1 %copy-start = (bf16[2,2,96,2048]{3,2,1,0:T(8,128)(2,1)S(1)}, bf16[2,2,96,2048]{3,2,1,0:T(8,128)(2,1)}, u32[]{:S(2)}) copy-start(bf16[2,2,96,2048]{3,2,1,0:T(8,128)(2,1)} %get-tuple-element.19.last) | copy-start | bytes 4718596
  274.5 5.1 %copy-start.1 = (bf16[2,32,2048]{2,1,0:T(8,128)(2,1)S(1)}, bf16[2,32,2048]{2,1,0:T(8,128)(2,1)}, u32[]{:S(2)}) copy-start(bf16[2,32,2048]{2,1,0:T(8,128)(2,1)} %get-tuple-element.26) | copy-start | bytes 786436
  277.6 2.1 collective-permute-start.3
  279.0 9.4 %collective-permute-start.5 = (bf16[2,112,2048]{2,1,0:T(8,128)(2,1)S(1)}, bf16[2,112,2048]{2,1,0:T(8,128)(2,1)S(1)}, u32[]{:S(2)}, u32[]{:S(2)}) collective-permute-start(bf16[2,112,2048]{2,1,0:T(8,128)(2,1)S(1)} %collective-permute-done.2.late_a1), channel_id=1, source_target_pairs={{0,1},{1,0},{2,3},{3,2},{4,5},{5,4},{6,7},{7,6},{8,9},{9,8},{10,11... | collective-permute-start | bytes 2752520 | tf_op jit(solution)/shard_map/ppermute | solution.py:515
  279.6 5.5 %collective-permute-start.4 = (bf16[2,32,2048]{2,1,0:T(8,128)(2,1)S(1)}, bf16[2,32,2048]{2,1,0:T(8,128)(2,1)S(1)}, u32[]{:S(2)}, u32[]{:S(2)}) collective-permute-start(bf16[2,32,2048]{2,1,0:T(8,128)(2,1)S(1)} %copy-done.1), channel_id=1, source_target_pairs={{0,2},{1,7},{2,4},{3,1},{4,6},{5,3},{6,0},{7,5},{8,10},{9,15},{10,... | collective-permute-start | bytes 786440 | tf_op jit(solution)/shard_map/ppermute | solution.py:482
  285.1 3.3 %collective-permute-start.6 = (bf16[2,32,2048]{2,1,0:T(8,128)(2,1)S(1)}, bf16[2,32,2048]{2,1,0:T(8,128)(2,1)S(1)}, u32[]{:S(2)}, u32[]{:S(2)}) collective-permute-start(bf16[2,32,2048]{2,1,0:T(8,128)(2,1)S(1)} %collective-permute-done.4.late_a2), channel_id=1, source_target_pairs={{0,1},{1,0},{2,3},{3,2},{4,5},{5,4},{6,7},{7,6},{8,9},{9,8},{10,11... | collective-permute-start | bytes 786440 | tf_op jit(solution)/shard_map/ppermute | solution.py:518
